TPU v7x, 128 devices: a whole 4x4x4 slice. The times are simulated.
128 devices in a mesh: blk: 128 (over y, x, z, core).
Axes of the slice: x: 4, y: 4, z: 4, core: 2. Of those that a mesh axis runs over, the one named last changes fastest.
Arguments:
- node_latent: bfloat16 [524288, 128], P('blk'), may hold values from -16 to 16
- edge_latent: bfloat16 [3145728, 128], P('blk'), may hold values from -6 to 6
- edge_ends: int32 [2, 3145728], P(None, 'blk'), may hold values from 0 to 5631, as said below
- edge_owned: int32 [3145728], P('blk'), may hold values from 0 to 1, as said below
- send_index: int32 [128, 6, 256], P('blk'), may hold values from 0 to 4095, as said below
- edge_w1: bfloat16 [2, 384, 128], replicated, may hold values from -0.3125 to 0.3125
- edge_b1: float32 [2, 128], replicated, may hold values from -3 to 3
- edge_w2: bfloat16 [2, 128, 128], replicated, may hold values from -0.5 to 0.5
- edge_gain: float32 [2, 128], replicated, may hold values from 0.5 to 1.5
- edge_shift: float32 [2, 128], replicated, may hold values from -2 to 2
- node_w1: bfloat16 [2, 256, 128], replicated, may hold values from -0.375 to 0.375
- node_b1: float32 [2, 128], replicated, may hold values from -3 to 3
- node_w2: bfloat16 [2, 128, 128], replicated, may hold values from -0.5 to 0.5
- node_gain: float32 [2, 128], replicated, may hold values from 0.5 to 1.5
- node_shift: float32 [2, 128], replicated, may hold values from -2 to 2
Outputs:
- node_out: bfloat16 [524288, 128], P('blk')
- edge_out: bfloat16 [3145728, 128], P('blk')
Inputs may be any that keep to these rules, and one draw needn't show every extreme that they name: edge_ends[0] holds each slot's sender, edge_ends[1] its receiver, as entries of the block's extended node list. Slot s of a block lies in tile t = s // 128; each of its ends is either an own node from (t // 6) * 128 to (t // 6 + 1) * 128 - 1 or a halo entry from 4096 + (t % 6) * 256 to 4096 + (t % 6 + 1) * 256 - 1; at most one end of a slot is a halo entry. `edge_owned`: in each block the slots with 1 come first; every block has at least 15360 of them. send_index[b, k] lists 256 distinct nodes of block b.
All inputs are finite; a program needn't handle non-finite values.
Results may differ from a plain program's by a relative error of at most 0.0085.
Values may be sent and summed in bfloat16 or wider, within the bound.
A program may use at most 128 MiB of HBM per device.

v0:
```python
import functools

import jax
import jax.numpy as jnp
from jax import lax
from jax.sharding import Mesh
from jax.sharding import PartitionSpec as P

LAYERS = 2
FACES = 6
GX = 4
GY = 4
BLK = ("blk_0", "blk_1", "blk_2", "blk_3")


def passed_along(block, axis, distance):
    devices = range(lax.axis_size(axis))
    route = [((i - distance) % len(devices), i) for i in devices]
    return lax.ppermute(block, axis, route)


def over_axes(shard, axes):
    return functools.reduce(lax.psum, axes, shard)


def row_norm(mixed):
    centre = mixed - jnp.mean(mixed, axis=1, keepdims=True)
    spread = jnp.mean(centre * centre, axis=1, keepdims=True)
    return centre * lax.rsqrt(spread + 1e-05)


def one_hots(ends, own_rows, halo_rows, tile_rows, dtype):
    groups = own_rows // tile_rows
    index = ends.reshape(groups, FACES, tile_rows)
    own_local = index - (jnp.arange(groups, dtype=jnp.int32) * tile_rows)[:, None, None]
    halo_local = index - own_rows - (jnp.arange(FACES, dtype=jnp.int32) * halo_rows)[None, :, None]
    own_hot = (own_local[..., None] == jnp.arange(tile_rows, dtype=jnp.int32)).astype(dtype)
    halo_hot = (halo_local[..., None] == jnp.arange(halo_rows, dtype=jnp.int32)).astype(dtype)
    return (own_hot, halo_hot)


def select_rows(hots, own_table, halo_table):
    own_hot, halo_hot = hots
    groups, faces, tile_rows, _ = own_hot.shape
    columns = own_table.shape[1]
    own_view = own_table.reshape(groups, tile_rows, columns)
    halo_view = halo_table.reshape(faces, halo_hot.shape[3], columns)
    picked = jnp.einsum(
        "bken,bnc->bkec", own_hot, own_view, preferred_element_type=jnp.float32, precision=None
    )
    picked = picked + jnp.einsum(
        "bkeh,khc->bkec", halo_hot, halo_view, preferred_element_type=jnp.float32, precision=None
    )
    return picked.reshape(groups * faces * tile_rows, columns)


def per_device(
    node_latent,
    edge_latent,
    edge_ends,
    edge_owned,
    send_index,
    edge_w1,
    edge_b1,
    edge_w2,
    edge_gain,
    edge_shift,
    node_w1,
    node_b1,
    node_w2,
    node_gain,
    node_shift,
):
    width = node_latent.shape[1]
    own_rows = node_latent.shape[0]
    halo_rows = send_index.shape[2]
    tile_rows = min(128, own_rows)
    groups = own_rows // tile_rows
    offsets = (1, -1, GX, -GX, GX * GY, -GX * GY)
    face_rows = send_index[0]
    flat_faces = face_rows.reshape(-1)
    owned = edge_owned.astype(jnp.float32)[:, None]
    total_nodes = own_rows * lax.axis_size(BLK)
    recv_hots = one_hots(edge_ends[1], own_rows, halo_rows, tile_rows, jnp.bfloat16)
    latents = node_latent
    edge_state = edge_latent
    for layer_id in range(LAYERS):
        w_first = edge_w1[layer_id]
        outgoing = latents[face_rows]
        arrived = [
            passed_along(outgoing[face_id], BLK, offsets[face_id]) for face_id in range(FACES)
        ]
        halo_table = jnp.concatenate(arrived, axis=0)
        send_hots = one_hots(edge_ends[0], own_rows, halo_rows, tile_rows, jnp.bfloat16)
        from_send = select_rows(send_hots, latents, halo_table).astype(jnp.bfloat16)
        from_recv = select_rows(recv_hots, latents, halo_table).astype(jnp.bfloat16)
        joined = jnp.concatenate([edge_state, from_send, from_recv], axis=1)
        before = jnp.dot(joined, w_first, preferred_element_type=jnp.float32)
        hidden = jax.nn.relu(before + edge_b1[layer_id]).astype(jnp.bfloat16)
        mixed = jnp.dot(hidden, edge_w2[layer_id], preferred_element_type=jnp.float32)
        normed = edge_gain[layer_id] * row_norm(mixed) + edge_shift[layer_id]
        edges_new = (edge_state.astype(jnp.float32) + owned * normed).astype(jnp.bfloat16)
        message = (
            (owned * edges_new.astype(jnp.float32))
            .astype(jnp.bfloat16)
            .reshape(groups, FACES, tile_rows, width)
        )
        own_sums = jnp.einsum(
            "bken,bkec->bnc", recv_hots[0], message, preferred_element_type=jnp.float32
        ).reshape(own_rows, width)
        halo_sums = jnp.einsum(
            "bkeh,bkec->khc", recv_hots[1], message, preferred_element_type=jnp.float32
        )
        returned = [
            passed_along(halo_sums[face_id].astype(jnp.bfloat16), BLK, -offsets[face_id]).astype(
                jnp.float32
            )
            for face_id in range(FACES)
        ]
        node_sums = own_sums.at[flat_faces].add(jnp.concatenate(returned, axis=0))
        aggregate = node_sums.astype(jnp.bfloat16)
        node_in = jnp.concatenate([latents, aggregate], axis=1)
        node_hidden = jax.nn.relu(
            jnp.dot(node_in, node_w1[layer_id], preferred_element_type=jnp.float32)
            + node_b1[layer_id]
        ).astype(jnp.bfloat16)
        update = jnp.dot(node_hidden, node_w2[layer_id], preferred_element_type=jnp.float32)
        sums, squares = (
            over_axes(jnp.sum(update, axis=0), BLK),
            over_axes(jnp.sum(update * update, axis=0), BLK),
        )
        centre_mean = sums / total_nodes
        variance = jnp.maximum(squares / total_nodes - centre_mean * centre_mean, 0.0)
        deviation = update - centre_mean
        latents = (
            latents.astype(jnp.float32)
            + node_gain[layer_id] * deviation * lax.rsqrt(variance + 1e-05)
            + node_shift[layer_id]
        ).astype(jnp.bfloat16)
        edge_state = edges_new
    return (latents, edge_state)


def solution(mesh):
    torus = Mesh(mesh.devices.reshape(4, 4, 4, 2), ("blk_0", "blk_1", "blk_2", "blk_3"))
    return jax.shard_map(
        per_device,
        mesh=torus,
        in_specs=(
            P(BLK, None),
            P(BLK, None),
            P(None, BLK),
            P(BLK),
            P(BLK, None, None),
            P(),
            P(),
            P(),
            P(),
            P(),
            P(),
            P(),
            P(),
            P(),
            P(),
        ),
        out_specs=(P(BLK, None), P(BLK, None)),
        check_vma=False,
    )
```

profile of v0, /device:TPU:1, one launch (start us, length us, event | category | flops | bytes accessed | tf_op | source)
XLA Modules:
  0.0 374.7 jit_solution(3821135400010055631)
XLA Ops:
  1.5 4.0 %gather_fusion = bf16[1536,128]{1,0:T(8,128)(2,1)S(1)} fusion(bf16[4096,128]{1,0:T(8,128)(2,1)} %param.15, s32[2048]{0:T(1024)S(1)} %pad_clamp_fusion), kind=kCustom, calls=%fused_computation | custom fusion | bytes 792576 | tf_op jit(solution)/shard_map/gather | solution.py:89
  5.5 6.1 %collective-permute-start.5 = (bf16[256,128]{1,0:T(8,128)(2,1)S(1)}, bf16[256,128]{1,0:T(8,128)(2,1)S(1)}, u32[]{:S(2)}, u32[]{:S(2)}) collective-permute-start(bf16[256,128]{1,0:T(8,128)(2,1)S(1)} %get-tuple-element.46), channel_id=1, source_target_pairs={{16,0},{17,1},{18,2},{19,3},{20,4},{21,5},{22,6},{23,7},{24,8},{25... | collective-permute-start | bytes 196616 | tf_op jit(solution)/shard_map/ppermute | solution.py:19
  11.6 8.1 %collective-permute-start.3 = (bf16[256,128]{1,0:T(8,128)(2,1)S(1)}, bf16[256,128]{1,0:T(8,128)(2,1)S(1)}, u32[]{:S(2)}, u32[]{:S(2)}) collective-permute-start(bf16[256,128]{1,0:T(8,128)(2,1)S(1)} %get-tuple-element.48), channel_id=1, source_target_pairs={{4,0},{5,1},{6,2},{7,3},{8,4},{9,5},{10,6},{11,7},{12,8},{13,9},{1... | collective-permute-start | bytes 196616 | tf_op jit(solution)/shard_map/ppermute | solution.py:19
  26.6 7.9 %fusion.33 = f32[32,6,128,128]{3,2,1,0:T(8,128)S(1)} fusion(bf16[32,128,128,1]{2,1,3,0:T(8,128)(2,1)S(1)} %bitcast.163, s32[32,6,128]{2,1,0:T(8,128)S(1)} %get-tuple-element.56), kind=kOutput, calls=%fused_computation.52 | convolution fusion | flops 808452096 | bytes 13729792 | tf_op jit(solution)/shard_map/bken,bnc->bkec/dot_general | solution.py:48
  34.5 3.4 fusion.37
  39.3 3.7 collective-permute-done.1
  43.1 8.2 %fusion.29 = bf16[32,6,128,128]{3,2,1,0:T(8,128)(2,1)} fusion(f32[32,6,128,128]{3,2,1,0:T(8,128)S(1)} %fusion.33, bf16[6,256,128,1]{2,1,0,3:T(8,128)(2,1)S(1)} %bitcast.172, s32[32,6,128]{2,0,1:T(8,128)S(1)} %copy.29), kind=kOutput, calls=%fused_computation.43 | convolution fusion | flops 1623195648 | bytes 19365888 | tf_op jit(solution)/shard_map/bkeh,khc->bkec/dot_general | solution.py:51
  51.4 8.8 %fusion.28 = bf16[32,6,128,128]{3,2,1,0:T(8,128)(2,1)} fusion(f32[32,6,128,128]{3,2,1,0:T(8,128)S(1)} %fusion.37, bf16[6,256,128,1]{2,1,0,3:T(8,128)(2,1)S(1)} %bitcast.173, s32[32,6,128]{2,0,1:T(8,128)S(1)} %copy.32), kind=kOutput, calls=%fused_computation.41 | convolution fusion | flops 1623195648 | bytes 19365888 | tf_op jit(solution)/shard_map/bkeh,khc->bkec/dot_general | solution.py:51
  60.2 14.5 %fusion.139 = (f32[24576]{0:T(1024)S(1)}, f32[24576,128]{1,0:T(8,128)}) fusion(bf16[2,128,128]{2,1,0:T(8,128)(2,1)S(1)} %copy-done.15, bf16[24576,128]{1,0:T(8,128)(2,1)} %bitcast.179, bf16[24576,128]{1,0:T(8,128)(2,1)} %bitcast.178, bf16[24576,128]{1,0:T(8,128)(2,1)} %param.16, f32[128]{0:T(128)S(1)} %get-tuple-element.67, ...), kind=kOutput, calls=%fused_computation.195 | convolution fusion | flops 3290406912 | bytes 31687168 | tf_op jit(solution)/shard_map/dot_general | solution.py:100
  74.7 10.3 %multiply_reduce_fusion.1 = f32[24576]{0:T(1024)S(1)} fusion(f32[24576,128]{1,0:T(8,128)} %get-tuple-element.75, f32[24576]{0:T(1024)S(1)} %broadcast_multiply_fusion.1), kind=kLoop, calls=%fused_computation.47 | loop fusion | flops 9412608 | bytes 12779520 | tf_op jit(solution)/shard_map/reduce_sum | solution.py:28
  85.0 22.2 %fusion.24 = (bf16[24576,128]{1,0:T(8,128)(2,1)S(1)}, bf16[24576,128]{1,0:T(8,128)(2,1)}) fusion(f32[24576]{0:T(1024)S(1)} %convert_element_type.146, f32[128]{0:T(128)S(1)} %get-tuple-element.81, f32[24576]{0:T(1024)S(1)} %add_rsqrt_fusion.1, f32[24576,128]{1,0:T(8,128)S(1)} %copy-done.1, f32[24576]{0:T(1024)S(1)} %broadcast_multiply_fusion.1, ...), kind=kLoop, calls=%fused_computation.34 | loop fusion | flops 34603008 | bytes 31753216 | tf_op jit(solution)/shard_map/convert_element_type | solution.py:105
  107.2 3.7 fusion.85
  111.0 5.2 %collective-permute-start.6 = (bf16[256,128]{1,0:T(8,128)(2,1)S(1)}, bf16[256,128]{1,0:T(8,128)(2,1)S(1)}, u32[]{:S(2)}, u32[]{:S(2)}) collective-permute-start(bf16[256,128]{1,0:T(8,128)(2,1)S(1)} %get-tuple-element.45), channel_id=1, source_target_pairs={{1,0},{2,1},{3,2},{4,3},{5,4},{6,5},{7,6},{8,7},{9,8},{10,9},{11,1... | collective-permute-start | bytes 196616 | tf_op jit(solution)/shard_map/ppermute | solution.py:19
  116.2 3.7 fusion.36
  119.9 5.1 %collective-permute-start.10 = (bf16[256,128]{1,0:T(8,128)(2,1)S(1)}, bf16[256,128]{1,0:T(8,128)(2,1)S(1)}, u32[]{:S(2)}, u32[]{:S(2)}) collective-permute-start(bf16[256,128]{1,0:T(8,128)(2,1)S(1)} %get-tuple-element.41), channel_id=1, source_target_pairs={{16,0},{17,1},{18,2},{19,3},{20,4},{21,5},{22,6},{23,7},{24,8},{25... | collective-permute-start | bytes 196616 | tf_op jit(solution)/shard_map/ppermute | solution.py:19
  125.0 7.2 %collective-permute-start.8 = (bf16[256,128]{1,0:T(8,128)(2,1)S(1)}, bf16[256,128]{1,0:T(8,128)(2,1)S(1)}, u32[]{:S(2)}, u32[]{:S(2)}) collective-permute-start(bf16[256,128]{1,0:T(8,128)(2,1)S(1)} %get-tuple-element.43), channel_id=1, source_target_pairs={{4,0},{5,1},{6,2},{7,3},{8,4},{9,5},{10,6},{11,7},{12,8},{13,9},{1... | collective-permute-start | bytes 196616 | tf_op jit(solution)/shard_map/ppermute | solution.py:19
  132.2 9.1 %collective-permute-done.7 = bf16[256,128]{1,0:T(8,128)(2,1)S(1)} collective-permute-done((bf16[256,128]{1,0:T(8,128)(2,1)S(1)}, bf16[256,128]{1,0:T(8,128)(2,1)S(1)}, u32[]{:S(2)}, u32[]{:S(2)}) %collective-permute-start.7) | collective-permute-done | bytes 65568 | tf_op jit(solution)/shard_map/ppermute | solution.py:19
  141.4 10.8 %scatter_custom_fusion = f32[4096,128]{1,0:T(8,128)} fusion(f32[4096,128]{1,0:T(8,128)} %bitcast.170, s32[1536]{0:T(1024)S(1)} %fusion.121, bf16[1536,128]{1,0:T(8,128)(2,1)S(1)} %constant_dynamic-update-slice_fusion.6), kind=kCustom, calls=%fused_computation.96 | custom fusion | flops 393216 | bytes 2490368 | tf_op jit(solution)/shard_map/scatter-add | solution.py:120
  153.9 2.6 fusion.135
  156.5 6.0 %all-reduce.5 = (f32[128]{0:T(128)S(1)}, f32[128]{0:T(128)S(1)}) all-reduce(f32[128]{0:T(128)S(1)} %get-tuple-element.5, f32[128]{0:T(128)S(1)} %get-tuple-element.4), channel_id=1, replica_groups=mesh['blk_0'=4,'blk_1'=4,'blk_2'=4,'blk_3'=2] {'blk_0'}, use_global_device_ids=true, to_apply=%region_9.10 | all-reduce | flops 256 | bytes 2048 | tf_op jit(solution)/shard_map/psum | solution.py:23
  162.5 6.0 %all-reduce.3 = (f32[128]{0:T(128)S(1)}, f32[128]{0:T(128)S(1)}) all-reduce(f32[128]{0:T(128)S(1)} %get-tuple-element.18, f32[128]{0:T(128)S(1)} %get-tuple-element.19), channel_id=1, replica_groups=mesh['blk_0'=4,'blk_1'=4,'blk_2'=4,'blk_3'=2] {'blk_1'}, use_global_device_ids=true, to_apply=%region_10.11 | all-reduce | flops 256 | bytes 2048 | tf_op jit(solution)/shard_map/psum | solution.py:23
  168.5 13.9 %all-reduce.1 = (f32[128]{0:T(128)S(1)}, f32[128]{0:T(128)S(1)}) all-reduce(f32[128]{0:T(128)S(1)} %get-tuple-element.14, f32[128]{0:T(128)S(1)} %get-tuple-element.15), channel_id=1, replica_groups=mesh['blk_0'=4,'blk_1'=4,'blk_2'=4,'blk_3'=2] {'blk_2'}, use_global_device_ids=true, to_apply=%region_11.12 | all-reduce | flops 256 | bytes 2048 | tf_op jit(solution)/shard_map/psum | solution.py:23
  182.4 7.8 %all-reduce.7 = (f32[128]{0:T(128)S(1)}, f32[128]{0:T(128)S(1)}) all-reduce(f32[128]{0:T(128)S(1)} %get-tuple-element.10, f32[128]{0:T(128)S(1)} %get-tuple-element.11), channel_id=1, replica_groups=mesh['blk_0'=4,'blk_1'=4,'blk_2'=4,'blk_3'=2] {'blk_3'}, use_global_device_ids=true, to_apply=%region_12.13 | all-reduce | flops 256 | bytes 2048 | tf_op jit(solution)/shard_map/psum | solution.py:23
  192.3 3.2 gather_fusion.1
  195.5 2.2 collective-permute-start.12
  197.7 7.8 %fusion.32 = f32[32,6,128,128]{3,2,1,0:T(8,128)S(1)} fusion(bf16[32,128,128,1]{2,1,3,0:T(8,128)(2,1)S(1)} %bitcast.161, s32[32,6,128]{2,1,0:T(8,128)S(1)} %get-tuple-element.56), kind=kOutput, calls=%fused_computation.51 | convolution fusion | flops 808452096 | bytes 13729792 | tf_op jit(solution)/shard_map/bken,bnc->bkec/dot_general | solution.py:48
  205.5 3.4 fusion.35
  208.9 2.4 collective-permute-start.17
  211.9 6.2 %collective-permute-start.15 = (bf16[256,128]{1,0:T(8,128)(2,1)S(1)}, bf16[256,128]{1,0:T(8,128)(2,1)S(1)}, u32[]{:S(2)}, u32[]{:S(2)}) collective-permute-start(bf16[256,128]{1,0:T(8,128)(2,1)S(1)} %get-tuple-element.36), channel_id=1, source_target_pairs={{4,0},{5,1},{6,2},{7,3},{8,4},{9,5},{10,6},{11,7},{12,8},{13,9},{1... | collective-permute-start | bytes 196616 | tf_op jit(solution)/shard_map/ppermute | solution.py:19
  218.2 4.0 %collective-permute-done.13 = bf16[256,128]{1,0:T(8,128)(2,1)S(1)} collective-permute-done((bf16[256,128]{1,0:T(8,128)(2,1)S(1)}, bf16[256,128]{1,0:T(8,128)(2,1)S(1)}, u32[]{:S(2)}, u32[]{:S(2)}) %collective-permute-start.13) | collective-permute-done | bytes 65568 | tf_op jit(solution)/shard_map/ppermute | solution.py:19
  222.2 5.1 %collective-permute-done.14 = bf16[256,128]{1,0:T(8,128)(2,1)S(1)} collective-permute-done((bf16[256,128]{1,0:T(8,128)(2,1)S(1)}, bf16[256,128]{1,0:T(8,128)(2,1)S(1)}, u32[]{:S(2)}, u32[]{:S(2)}) %collective-permute-start.14) | collective-permute-done | bytes 65568 | tf_op jit(solution)/shard_map/ppermute | solution.py:19
  227.3 8.3 %fusion.27 = bf16[32,6,128,128]{3,2,1,0:T(8,128)(2,1)} fusion(f32[32,6,128,128]{3,2,1,0:T(8,128)S(1)} %fusion.32, bf16[6,256,128,1]{2,1,0,3:T(8,128)(2,1)S(1)} %bitcast.174, s32[32,6,128]{2,0,1:T(8,128)S(1)} %copy.29), kind=kOutput, calls=%fused_computation.39 | convolution fusion | flops 1623195648 | bytes 19365888 | tf_op jit(solution)/shard_map/bkeh,khc->bkec/dot_general | solution.py:51
  235.6 8.8 %fusion.26 = bf16[32,6,128,128]{3,2,1,0:T(8,128)(2,1)} fusion(f32[32,6,128,128]{3,2,1,0:T(8,128)S(1)} %fusion.35, bf16[6,256,128,1]{2,1,0,3:T(8,128)(2,1)S(1)} %bitcast.175, s32[32,6,128]{2,0,1:T(8,128)S(1)} %copy.32), kind=kOutput, calls=%fused_computation.37 | convolution fusion | flops 1623195648 | bytes 19365888 | tf_op jit(solution)/shard_map/bkeh,khc->bkec/dot_general | solution.py:51
  244.4 14.5 %fusion.148 = (f32[24576]{0:T(1024)S(1)}, f32[24576,128]{1,0:T(8,128)}) fusion(bf16[2,128,128]{2,1,0:T(8,128)(2,1)S(1)} %copy-done.15, bf16[24576,128]{1,0:T(8,128)(2,1)} %bitcast.177, bf16[24576,128]{1,0:T(8,128)(2,1)} %bitcast.176, bf16[24576,128]{1,0:T(8,128)(2,1)} %get-tuple-element.27, f32[128]{0:T(128)S(1)} %get-tuple-element.66, ...), kind=kOutput, calls=%fused_computation.196 | convolution fusion | flops 3290406912 | bytes 31687168 | tf_op jit(solution)/shard_map/dot_general | solution.py:100
  258.9 10.7 %multiply_reduce_fusion = f32[24576]{0:T(1024)S(1)} fusion(f32[24576,128]{1,0:T(8,128)} %get-tuple-element.78, f32[24576]{0:T(1024)S(1)} %broadcast_multiply_fusion), kind=kLoop, calls=%fused_computation.45 | loop fusion | flops 9412608 | bytes 12779520 | tf_op jit(solution)/shard_map/reduce_sum | solution.py:28
  269.7 22.2 %multiply_convert_fusion = (bf16[24576,128]{1,0:T(8,128)(2,1)S(1)}, bf16[24576,128]{1,0:T(8,128)(2,1)}) fusion(f32[24576]{0:T(1024)S(1)} %convert_element_type.146, f32[128]{0:T(128)S(1)} %copy-done.7, f32[24576]{0:T(1024)S(1)} %add_rsqrt_fusion, f32[24576,128]{1,0:T(8,128)S(1)} %copy-done, f32[24576]{0:T(1024)S(1)} %broadcast_multiply_fusion, ...), kind=kLoop, calls=%fused_computation.44 | loop fusion | flops 34603008 | bytes 31753216 | tf_op jit(solution)/shard_map/convert_element_type | solution.py:105
  291.9 3.7 fusion.82
  297.4 3.7 fusion.34
  301.1 5.1 %collective-permute-start.22 = (bf16[256,128]{1,0:T(8,128)(2,1)S(1)}, bf16[256,128]{1,0:T(8,128)(2,1)S(1)}, u32[]{:S(2)}, u32[]{:S(2)}) collective-permute-start(bf16[256,128]{1,0:T(8,128)(2,1)S(1)} %get-tuple-element.29), channel_id=1, source_target_pairs={{16,0},{17,1},{18,2},{19,3},{20,4},{21,5},{22,6},{23,7},{24,8},{25... | collective-permute-start | bytes 196616 | tf_op jit(solution)/shard_map/ppermute | solution.py:19
  306.2 7.2 %collective-permute-start.20 = (bf16[256,128]{1,0:T(8,128)(2,1)S(1)}, bf16[256,128]{1,0:T(8,128)(2,1)S(1)}, u32[]{:S(2)}, u32[]{:S(2)}) collective-permute-start(bf16[256,128]{1,0:T(8,128)(2,1)S(1)} %get-tuple-element.31), channel_id=1, source_target_pairs={{4,0},{5,1},{6,2},{7,3},{8,4},{9,5},{10,6},{11,7},{12,8},{13,9},{1... | collective-permute-start | bytes 196616 | tf_op jit(solution)/shard_map/ppermute | solution.py:19
  314.7 7.7 %collective-permute-done.19 = bf16[256,128]{1,0:T(8,128)(2,1)S(1)} collective-permute-done((bf16[256,128]{1,0:T(8,128)(2,1)S(1)}, bf16[256,128]{1,0:T(8,128)(2,1)S(1)}, u32[]{:S(2)}, u32[]{:S(2)}) %collective-permute-start.19) | collective-permute-done | bytes 65568 | tf_op jit(solution)/shard_map/ppermute | solution.py:19
  322.6 10.8 %scatter_custom_fusion.1 = f32[4096,128]{1,0:T(8,128)} fusion(f32[4096,128]{1,0:T(8,128)} %bitcast.169, s32[1536]{0:T(1024)S(1)} %fusion.121, bf16[1536,128]{1,0:T(8,128)(2,1)S(1)} %constant_dynamic-update-slice_fusion.18), kind=kCustom, calls=%fused_computation.94 | custom fusion | flops 393216 | bytes 2490368 | tf_op jit(solution)/shard_map/scatter-add | solution.py:120
  335.1 2.6 fusion.134
  337.7 6.0 %all-reduce.4 = (f32[128]{0:T(128)S(1)}, f32[128]{0:T(128)S(1)}) all-reduce(f32[128]{0:T(128)S(1)} %get-tuple-element.3, f32[128]{0:T(128)S(1)} %get-tuple-element.2), channel_id=1, replica_groups=mesh['blk_0'=4,'blk_1'=4,'blk_2'=4,'blk_3'=2] {'blk_0'}, use_global_device_ids=true, to_apply=%region_22.23 | all-reduce | flops 256 | bytes 2048 | tf_op jit(solution)/shard_map/psum | solution.py:23
  343.7 6.0 %all-reduce.2 = (f32[128]{0:T(128)S(1)}, f32[128]{0:T(128)S(1)}) all-reduce(f32[128]{0:T(128)S(1)} %get-tuple-element.16, f32[128]{0:T(128)S(1)} %get-tuple-element.17), channel_id=1, replica_groups=mesh['blk_0'=4,'blk_1'=4,'blk_2'=4,'blk_3'=2] {'blk_1'}, use_global_device_ids=true, to_apply=%region_23.24 | all-reduce | flops 256 | bytes 2048 | tf_op jit(solution)/shard_map/psum | solution.py:23
  349.7 13.9 %all-reduce = (f32[128]{0:T(128)S(1)}, f32[128]{0:T(128)S(1)}) all-reduce(f32[128]{0:T(128)S(1)} %get-tuple-element.12, f32[128]{0:T(128)S(1)} %get-tuple-element.13), channel_id=1, replica_groups=mesh['blk_0'=4,'blk_1'=4,'blk_2'=4,'blk_3'=2] {'blk_2'}, use_global_device_ids=true, to_apply=%region_24.25 | all-reduce | flops 256 | bytes 2048 | tf_op jit(solution)/shard_map/psum | solution.py:23
  363.6 7.8 %all-reduce.6 = (f32[128]{0:T(128)S(1)}, f32[128]{0:T(128)S(1)}) all-reduce(f32[128]{0:T(128)S(1)} %get-tuple-element.8, f32[128]{0:T(128)S(1)} %get-tuple-element.9), channel_id=1, replica_groups=mesh['blk_0'=4,'blk_1'=4,'blk_2'=4,'blk_3'=2] {'blk_3'}, use_global_device_ids=true, to_apply=%region_25.26 | all-reduce | flops 256 | bytes 2048 | tf_op jit(solution)/shard_map/psum | solution.py:23
  371.4 3.0 add_convert_fusion.1
  (121 shorter events, 18.8 us)
Async XLA Ops:
  0.6 25.9 %copy-start.2 = (bf16[4096,128]{1,0:T(8,128)(2,1)S(1)}, bf16[4096,128]{1,0:T(8,128)(2,1)}, u32[]{:S(2)}) copy-start(bf16[4096,128]{1,0:T(8,128)(2,1)} %param.15) | copy-start | bytes 3145732
  5.5 37.6 %collective-permute-start.5 = (bf16[256,128]{1,0:T(8,128)(2,1)S(1)}, bf16[256,128]{1,0:T(8,128)(2,1)S(1)}, u32[]{:S(2)}, u32[]{:S(2)}) collective-permute-start(bf16[256,128]{1,0:T(8,128)(2,1)S(1)} %get-tuple-element.46), channel_id=1, source_target_pairs={{16,0},{17,1},{18,2},{19,3},{20,4},{21,5},{22,6},{23,7},{24,8},{25... | collective-permute-start | bytes 196616 | tf_op jit(solution)/shard_map/ppermute | solution.py:19
  11.6 31.5 %collective-permute-start.4 = (bf16[256,128]{1,0:T(8,128)(2,1)S(1)}, bf16[256,128]{1,0:T(8,128)(2,1)S(1)}, u32[]{:S(2)}, u32[]{:S(2)}) collective-permute-start(bf16[256,128]{1,0:T(8,128)(2,1)S(1)} %get-tuple-element.47), channel_id=1, source_target_pairs={{112,0},{113,1},{114,2},{115,3},{116,4},{117,5},{118,6},{119,7},{1... | collective-permute-start | bytes 196616 | tf_op jit(solution)/shard_map/ppermute | solution.py:19
  11.6 31.4 %collective-permute-start.3 = (bf16[256,128]{1,0:T(8,128)(2,1)S(1)}, bf16[256,128]{1,0:T(8,128)(2,1)S(1)}, u32[]{:S(2)}, u32[]{:S(2)}) collective-permute-start(bf16[256,128]{1,0:T(8,128)(2,1)S(1)} %get-tuple-element.48), channel_id=1, source_target_pairs={{4,0},{5,1},{6,2},{7,3},{8,4},{9,5},{10,6},{11,7},{12,8},{13,9},{1... | collective-permute-start | bytes 196616 | tf_op jit(solution)/shard_map/ppermute | solution.py:19
  19.7 23.3 %collective-permute-start.2 = (bf16[256,128]{1,0:T(8,128)(2,1)S(1)}, bf16[256,128]{1,0:T(8,128)(2,1)S(1)}, u32[]{:S(2)}, u32[]{:S(2)}) collective-permute-start(bf16[256,128]{1,0:T(8,128)(2,1)S(1)} %get-tuple-element.49), channel_id=1, source_target_pairs={{124,0},{125,1},{126,2},{127,3},{0,4},{1,5},{2,6},{3,7},{4,8},{5,9... | collective-permute-start | bytes 196616 | tf_op jit(solution)/shard_map/ppermute | solution.py:19
  19.7 19.3 %collective-permute-start = (bf16[256,128]{1,0:T(8,128)(2,1)S(1)}, bf16[256,128]{1,0:T(8,128)(2,1)S(1)}, u32[]{:S(2)}, u32[]{:S(2)}) collective-permute-start(bf16[256,128]{1,0:T(8,128)(2,1)S(1)} %get-tuple-element.51), channel_id=1, source_target_pairs={{127,0},{0,1},{1,2},{2,3},{3,4},{4,5},{5,6},{6,7},{7,8},{8,9},{9,1... | collective-permute-start | bytes 196616 | tf_op jit(solution)/shard_map/ppermute | solution.py:19
  34.4 3.5 copy-start.8
  34.4 3.5 copy-start.9
  34.4 4.0 %copy-start.10 = (f32[2,128]{1,0:T(2,128)S(1)}, f32[2,128]{1,0:T(2,128)}, u32[]{:S(2)}) copy-start(f32[2,128]{1,0:T(2,128)} %param.29) | copy-start | bytes 3076
  34.5 4.0 %copy-start.11 = (f32[2,128]{1,0:T(2,128)S(1)}, f32[2,128]{1,0:T(2,128)}, u32[]{:S(2)}) copy-start(f32[2,128]{1,0:T(2,128)} %param.28) | copy-start | bytes 3076
  34.5 4.5 %copy-start.3 = (s32[1,6,256]{2,0,1:T(1,128)S(1)}, s32[1,6,256]{2,0,1:T(1,128)}, u32[]{:S(2)}) copy-start(s32[1,6,256]{2,0,1:T(1,128)} %param.19) | copy-start | bytes 18436
  39.1 3.9 %collective-permute-start.1 = (bf16[256,128]{1,0:T(8,128)(2,1)S(1)}, bf16[256,128]{1,0:T(8,128)(2,1)S(1)}, u32[]{:S(2)}, u32[]{:S(2)}) collective-permute-start(bf16[256,128]{1,0:T(8,128)(2,1)S(1)} %get-tuple-element.50), channel_id=1, source_target_pairs={{1,0},{2,1},{3,2},{4,3},{5,4},{6,5},{7,6},{8,7},{9,8},{10,9},{11,1... | collective-permute-start | bytes 196616 | tf_op jit(solution)/shard_map/ppermute | solution.py:19
  51.4 8.8 %copy-start.13 = (bf16[2,384,128]{2,1,0:T(8,128)(2,1)S(1)}, bf16[2,384,128]{2,1,0:T(8,128)(2,1)}, u32[]{:S(2)}) copy-start(bf16[2,384,128]{2,1,0:T(8,128)(2,1)} %param.20) | copy-start | bytes 589828
  51.4 8.8 %copy-start.15 = (bf16[2,128,128]{2,1,0:T(8,128)(2,1)S(1)}, bf16[2,128,128]{2,1,0:T(8,128)(2,1)}, u32[]{:S(2)}) copy-start(bf16[2,128,128]{2,1,0:T(8,128)(2,1)} %param.22) | copy-start | bytes 196612
  74.7 10.3 %copy-start.1 = (f32[24576,128]{1,0:T(8,128)S(1)}, f32[24576,128]{1,0:T(8,128)}, u32[]{:S(2)}) copy-start(f32[24576,128]{1,0:T(8,128)} %get-tuple-element.75) | copy-start | bytes 37748740
  111.0 21.2 %collective-permute-start.6 = (bf16[256,128]{1,0:T(8,128)(2,1)S(1)}, bf16[256,128]{1,0:T(8,128)(2,1)S(1)}, u32[]{:S(2)}, u32[]{:S(2)}) collective-permute-start(bf16[256,128]{1,0:T(8,128)(2,1)S(1)} %get-tuple-element.45), channel_id=1, source_target_pairs={{1,0},{2,1},{3,2},{4,3},{5,4},{6,5},{7,6},{8,7},{9,8},{10,9},{11,1... | collective-permute-start | bytes 196616 | tf_op jit(solution)/shard_map/ppermute | solution.py:19
  119.9 34.0 %copy-start.14 = (bf16[2,256,128]{2,1,0:T(8,128)(2,1)S(1)}, bf16[2,256,128]{2,1,0:T(8,128)(2,1)}, u32[]{:S(2)}) copy-start(bf16[2,256,128]{2,1,0:T(8,128)(2,1)} %param.25) | copy-start | bytes 393220
  119.9 34.0 %copy-start.16 = (bf16[2,128,128]{2,1,0:T(8,128)(2,1)S(1)}, bf16[2,128,128]{2,1,0:T(8,128)(2,1)}, u32[]{:S(2)}) copy-start(bf16[2,128,128]{2,1,0:T(8,128)(2,1)} %param.27) | copy-start | bytes 196612
  119.9 21.5 %collective-permute-start.11 = (bf16[256,128]{1,0:T(8,128)(2,1)S(1)}, bf16[256,128]{1,0:T(8,128)(2,1)S(1)}, u32[]{:S(2)}, u32[]{:S(2)}) collective-permute-start(bf16[256,128]{1,0:T(8,128)(2,1)S(1)} %get-tuple-element.40), channel_id=1, source_target_pairs={{112,0},{113,1},{114,2},{115,3},{116,4},{117,5},{118,6},{119,7},{1... | collective-permute-start | bytes 196616 | tf_op jit(solution)/shard_map/ppermute | solution.py:19
  119.9 21.4 %collective-permute-start.10 = (bf16[256,128]{1,0:T(8,128)(2,1)S(1)}, bf16[256,128]{1,0:T(8,128)(2,1)S(1)}, u32[]{:S(2)}, u32[]{:S(2)}) collective-permute-start(bf16[256,128]{1,0:T(8,128)(2,1)S(1)} %get-tuple-element.41), channel_id=1, source_target_pairs={{16,0},{17,1},{18,2},{19,3},{20,4},{21,5},{22,6},{23,7},{24,8},{25... | collective-permute-start | bytes 196616 | tf_op jit(solution)/shard_map/ppermute | solution.py:19
  125.0 16.3 %collective-permute-start.9 = (bf16[256,128]{1,0:T(8,128)(2,1)S(1)}, bf16[256,128]{1,0:T(8,128)(2,1)S(1)}, u32[]{:S(2)}, u32[]{:S(2)}) collective-permute-start(bf16[256,128]{1,0:T(8,128)(2,1)S(1)} %get-tuple-element.42), channel_id=1, source_target_pairs={{124,0},{125,1},{126,2},{127,3},{0,4},{1,5},{2,6},{3,7},{4,8},{5,9... | collective-permute-start | bytes 196616 | tf_op jit(solution)/shard_map/ppermute | solution.py:19
  125.0 16.3 %collective-permute-start.8 = (bf16[256,128]{1,0:T(8,128)(2,1)S(1)}, bf16[256,128]{1,0:T(8,128)(2,1)S(1)}, u32[]{:S(2)}, u32[]{:S(2)}) collective-permute-start(bf16[256,128]{1,0:T(8,128)(2,1)S(1)} %get-tuple-element.43), channel_id=1, source_target_pairs={{4,0},{5,1},{6,2},{7,3},{8,4},{9,5},{10,6},{11,7},{12,8},{13,9},{1... | collective-permute-start | bytes 196616 | tf_op jit(solution)/shard_map/ppermute | solution.py:19
  132.2 9.1 %collective-permute-start.7 = (bf16[256,128]{1,0:T(8,128)(2,1)S(1)}, bf16[256,128]{1,0:T(8,128)(2,1)S(1)}, u32[]{:S(2)}, u32[]{:S(2)}) collective-permute-start(bf16[256,128]{1,0:T(8,128)(2,1)S(1)} %get-tuple-element.44), channel_id=1, source_target_pairs={{127,0},{0,1},{1,2},{2,3},{3,4},{4,5},{5,6},{6,7},{7,8},{8,9},{9,1... | collective-permute-start | bytes 196616 | tf_op jit(solution)/shard_map/ppermute | solution.py:19
  195.5 22.6 %collective-permute-start.12 = (bf16[256,128]{1,0:T(8,128)(2,1)S(1)}, bf16[256,128]{1,0:T(8,128)(2,1)S(1)}, u32[]{:S(2)}, u32[]{:S(2)}) collective-permute-start(bf16[256,128]{1,0:T(8,128)(2,1)S(1)} %get-tuple-element.39), channel_id=1, source_target_pairs={{127,0},{0,1},{1,2},{2,3},{3,4},{4,5},{5,6},{6,7},{7,8},{8,9},{9,1... | collective-permute-start | bytes 196616 | tf_op jit(solution)/shard_map/ppermute | solution.py:19
  208.9 18.4 %collective-permute-start.17 = (bf16[256,128]{1,0:T(8,128)(2,1)S(1)}, bf16[256,128]{1,0:T(8,128)(2,1)S(1)}, u32[]{:S(2)}, u32[]{:S(2)}) collective-permute-start(bf16[256,128]{1,0:T(8,128)(2,1)S(1)} %get-tuple-element.34), channel_id=1, source_target_pairs={{16,0},{17,1},{18,2},{19,3},{20,4},{21,5},{22,6},{23,7},{24,8},{25... | collective-permute-start | bytes 196616 | tf_op jit(solution)/shard_map/ppermute | solution.py:19
  211.3 16.0 %collective-permute-start.16 = (bf16[256,128]{1,0:T(8,128)(2,1)S(1)}, bf16[256,128]{1,0:T(8,128)(2,1)S(1)}, u32[]{:S(2)}, u32[]{:S(2)}) collective-permute-start(bf16[256,128]{1,0:T(8,128)(2,1)S(1)} %get-tuple-element.35), channel_id=1, source_target_pairs={{112,0},{113,1},{114,2},{115,3},{116,4},{117,5},{118,6},{119,7},{1... | collective-permute-start | bytes 196616 | tf_op jit(solution)/shard_map/ppermute | solution.py:19
  211.9 15.3 %collective-permute-start.15 = (bf16[256,128]{1,0:T(8,128)(2,1)S(1)}, bf16[256,128]{1,0:T(8,128)(2,1)S(1)}, u32[]{:S(2)}, u32[]{:S(2)}) collective-permute-start(bf16[256,128]{1,0:T(8,128)(2,1)S(1)} %get-tuple-element.36), channel_id=1, source_target_pairs={{4,0},{5,1},{6,2},{7,3},{8,4},{9,5},{10,6},{11,7},{12,8},{13,9},{1... | collective-permute-start | bytes 196616 | tf_op jit(solution)/shard_map/ppermute | solution.py:19
  218.1 9.1 %collective-permute-start.14 = (bf16[256,128]{1,0:T(8,128)(2,1)S(1)}, bf16[256,128]{1,0:T(8,128)(2,1)S(1)}, u32[]{:S(2)}, u32[]{:S(2)}) collective-permute-start(bf16[256,128]{1,0:T(8,128)(2,1)S(1)} %get-tuple-element.37), channel_id=1, source_target_pairs={{124,0},{125,1},{126,2},{127,3},{0,4},{1,5},{2,6},{3,7},{4,8},{5,9... | collective-permute-start | bytes 196616 | tf_op jit(solution)/shard_map/ppermute | solution.py:19
  218.1 4.0 %collective-permute-start.13 = (bf16[256,128]{1,0:T(8,128)(2,1)S(1)}, bf16[256,128]{1,0:T(8,128)(2,1)S(1)}, u32[]{:S(2)}, u32[]{:S(2)}) collective-permute-start(bf16[256,128]{1,0:T(8,128)(2,1)S(1)} %get-tuple-element.38), channel_id=1, source_target_pairs={{1,0},{2,1},{3,2},{4,3},{5,4},{6,5},{7,6},{8,7},{9,8},{10,9},{11,1... | collective-permute-start | bytes 196616 | tf_op jit(solution)/shard_map/ppermute | solution.py:19
  258.9 10.7 %copy-start = (f32[24576,128]{1,0:T(8,128)S(1)}, f32[24576,128]{1,0:T(8,128)}, u32[]{:S(2)}) copy-start(f32[24576,128]{1,0:T(8,128)} %get-tuple-element.78) | copy-start | bytes 37748740
  258.9 10.7 %copy-start.6 = (f32[128]{0:T(128)S(1)}, f32[128]{0:T(128)}, u32[]{:S(2)}) copy-start(f32[128]{0:T(128)} %get-tuple-element.64) | copy-start | bytes 1540
  258.9 10.7 %copy-start.7 = (f32[128]{0:T(128)S(1)}, f32[128]{0:T(128)}, u32[]{:S(2)}) copy-start(f32[128]{0:T(128)} %get-tuple-element.80) | copy-start | bytes 1540
  295.7 17.7 %collective-permute-start.18 = (bf16[256,128]{1,0:T(8,128)(2,1)S(1)}, bf16[256,128]{1,0:T(8,128)(2,1)S(1)}, u32[]{:S(2)}, u32[]{:S(2)}) collective-permute-start(bf16[256,128]{1,0:T(8,128)(2,1)S(1)} %get-tuple-element.33), channel_id=1, source_target_pairs={{1,0},{2,1},{3,2},{4,3},{5,4},{6,5},{7,6},{8,7},{9,8},{10,9},{11,1... | collective-permute-start | bytes 196616 | tf_op jit(solution)/shard_map/ppermute | solution.py:19
  301.1 34.0 %copy-start.12 = (f32[128]{0:T(128)S(1)}, f32[128]{0:T(128)}, u32[]{:S(2)}) copy-start(f32[128]{0:T(128)} %get-tuple-element.62) | copy-start | bytes 1540
  301.1 21.5 %collective-permute-start.23 = (bf16[256,128]{1,0:T(8,128)(2,1)S(1)}, bf16[256,128]{1,0:T(8,128)(2,1)S(1)}, u32[]{:S(2)}, u32[]{:S(2)}) collective-permute-start(bf16[256,128]{1,0:T(8,128)(2,1)S(1)} %get-tuple-element.28), channel_id=1, source_target_pairs={{112,0},{113,1},{114,2},{115,3},{116,4},{117,5},{118,6},{119,7},{1... | collective-permute-start | bytes 196616 | tf_op jit(solution)/shard_map/ppermute | solution.py:19
  301.1 21.4 %collective-permute-start.22 = (bf16[256,128]{1,0:T(8,128)(2,1)S(1)}, bf16[256,128]{1,0:T(8,128)(2,1)S(1)}, u32[]{:S(2)}, u32[]{:S(2)}) collective-permute-start(bf16[256,128]{1,0:T(8,128)(2,1)S(1)} %get-tuple-element.29), channel_id=1, source_target_pairs={{16,0},{17,1},{18,2},{19,3},{20,4},{21,5},{22,6},{23,7},{24,8},{25... | collective-permute-start | bytes 196616 | tf_op jit(solution)/shard_map/ppermute | solution.py:19
  306.2 16.3 %collective-permute-start.21 = (bf16[256,128]{1,0:T(8,128)(2,1)S(1)}, bf16[256,128]{1,0:T(8,128)(2,1)S(1)}, u32[]{:S(2)}, u32[]{:S(2)}) collective-permute-start(bf16[256,128]{1,0:T(8,128)(2,1)S(1)} %get-tuple-element.30), channel_id=1, source_target_pairs={{124,0},{125,1},{126,2},{127,3},{0,4},{1,5},{2,6},{3,7},{4,8},{5,9... | collective-permute-start | bytes 196616 | tf_op jit(solution)/shard_map/ppermute | solution.py:19
  306.2 16.3 %collective-permute-start.20 = (bf16[256,128]{1,0:T(8,128)(2,1)S(1)}, bf16[256,128]{1,0:T(8,128)(2,1)S(1)}, u32[]{:S(2)}, u32[]{:S(2)}) collective-permute-start(bf16[256,128]{1,0:T(8,128)(2,1)S(1)} %get-tuple-element.31), channel_id=1, source_target_pairs={{4,0},{5,1},{6,2},{7,3},{8,4},{9,5},{10,6},{11,7},{12,8},{13,9},{1... | collective-permute-start | bytes 196616 | tf_op jit(solution)/shard_map/ppermute | solution.py:19
  313.4 9.1 %collective-permute-start.19 = (bf16[256,128]{1,0:T(8,128)(2,1)S(1)}, bf16[256,128]{1,0:T(8,128)(2,1)S(1)}, u32[]{:S(2)}, u32[]{:S(2)}) collective-permute-start(bf16[256,128]{1,0:T(8,128)(2,1)S(1)} %get-tuple-element.32), channel_id=1, source_target_pairs={{127,0},{0,1},{1,2},{2,3},{3,4},{4,5},{5,6},{6,7},{7,8},{8,9},{9,1... | collective-permute-start | bytes 196616 | tf_op jit(solution)/shard_map/ppermute | solution.py:19
  322.6 48.8 %copy-start.4 = (f32[128]{0:T(128)S(1)}, f32[128]{0:T(128)}, u32[]{:S(2)}) copy-start(f32[128]{0:T(128)} %get-tuple-element.60) | copy-start | bytes 1540
  322.6 48.8 %copy-start.5 = (f32[128]{0:T(128)S(1)}, f32[128]{0:T(128)}, u32[]{:S(2)}) copy-start(f32[128]{0:T(128)} %get-tuple-element.83) | copy-start | bytes 1540
where the time goes:
time: 381 us; the launch traced here: 375 us
  matrix products  106 us (28%)
  other arithmetic  97.5 us (26%)
  blocking collectives  67.3 us (18%)
  starting transfers between devices  61 us (16%)
  waiting for transfers between devices  29.6 us (8%)
  local copies, waits for them, and re-layouts  12.4 us (3%)
    psum x8, blocking collectives, over_axes(): return functools.reduce(lax.psum, axes, shard)  67.3 us
    ppermute x24, starting transfers between devices, passed_along(): return lax.ppermute(block, axis, route)  61 us
    convert_element_type x2, other arithmetic, per_device(): message = (owned * edges_new.astype(jnp.float32)).astype(jnp.bfloat16).re...  44.4 us
    dot_general x4, matrix products, select_rows(): jnp.einsum('bkeh,khc->bkec', halo_hot, halo_view, preferred_element_type=...  34.1 us
    ppermute x24, waiting for transfers between devices, passed_along(): return lax.ppermute(block, axis, route)  29.6 us
    dot_general x2, matrix products, per_device(): jnp.dot(hidden, edge_w2[layer_id], preferred_element_type=jnp.float32)  28.9 us
    dot_general x4, matrix products, select_rows(): jnp.einsum('bken,bnc->bkec', own_hot, own_view, preferred_element_type=jn...  22.5 us
    scatter-add x2, other arithmetic, per_device(): node_sums = own_sums.at[flat_faces].add(jnp.concatenate(returned, axis=0))  21.7 us
  transfers between devices with their start and end apart: 24, of which 5 were waited for; matrix products, arithmetic and copies ran while one was open for 10% of the time, Pallas kernels for 0%

commit v1 on v0

v1 whole, which is shorter than its diff:
```python
import functools

import jax
import jax.numpy as jnp
from jax import lax
from jax.experimental import pallas as pl
from jax.experimental.pallas import tpu as pltpu
from jax.sharding import PartitionSpec as P

MESH = pl.DeviceIdType.MESH
F32 = jnp.float32
BF16 = jnp.bfloat16
LAYERS = 2
FACES = 6
PAIRS = 3
T = 128
H = 256
GB = 4
REF = 16
ROWS = 512


def dot(a, b):
    return jnp.dot(a, b, preferred_element_type=F32)


def dot_t(a, b):
    return lax.dot_general(a, b, (((1,), (1,)), ((), ())), preferred_element_type=F32)


def columns(row):
    return jnp.broadcast_to(row, (T, T)).T


def hot(index, rows):
    lanes = index.shape[1]
    code = jnp.broadcast_to(index, (16, lanes)).astype(jnp.int16)
    line = lax.broadcasted_iota(jnp.int32, (rows, lanes), 0).astype(jnp.int16)
    same = line.reshape(rows // 16, 16, lanes) == code[None]
    return jnp.where(same, jnp.ones((), BF16), jnp.zeros((), BF16)).reshape(rows, lanes)


def kernel(
    n_dev,
    groups,
    node_ref,
    edge_hbm,
    ends_ref,
    owned_ref,
    send_smem,
    send_ref,
    ew1,
    eb1,
    ew2,
    eg,
    es,
    nw1,
    nb1,
    nw2,
    ng,
    ns,
    node_out,
    edge_out,
    a_buf,
    b_buf,
    hb,
    rowsrc,
    agg,
    tab,
    htab,
    hid,
    ohr,
    ohh,
    hsum,
    stage,
    tx0,
    tx1,
    rx0,
    rx1,
    ret_tx,
    ret_rx,
    w_t,
    cols,
    st_tx,
    st_a,
    st_b,
    in_sem,
    out_sem,
    h_send,
    h_recv,
    r_send,
    r_recv,
    a_send,
    a_recv,
    b_send,
    b_recv,
):
    me = lax.axis_index("blk")
    nodes = groups * T
    blocks = groups // GB
    low, high = lax.rem(me, 8), lax.div(me, 8)
    n_high = n_dev // 8
    offsets = (1, n_dev - 1, 4, n_dev - 4, 16, n_dev - 16)

    def ahead(distance):
        return lax.rem(me + distance, n_dev)

    def partner_a(step):
        return high * 8 + lax.rem(low + step, 8)

    def partner_b(step):
        return lax.rem(high + step, n_high) * 8 + low

    def in_copy(pair, block):
        where = (pl.ds(block * GB, GB), pl.ds(pair * 2, 2))
        return pltpu.make_async_copy(
            edge_hbm.at[where], a_buf.at[where], in_sem.at[pair * blocks + block]
        )

    def out_copy(pair, block):
        where = (pl.ds(block * GB, GB), pl.ds(pair * 2, 2))
        return pltpu.make_async_copy(
            a_buf.at[where], edge_out.at[where], out_sem.at[pair * blocks + block]
        )

    def halo_copy(layer, face):
        source, target = ((tx0, rx0), (tx1, rx1))[layer]
        return pltpu.make_async_remote_copy(
            src_ref=source.at[face],
            dst_ref=target.at[face],
            send_sem=h_send.at[layer, face],
            recv_sem=h_recv.at[layer, face],
            device_id=(ahead(offsets[face]),),
            device_id_type=MESH,
        )

    def return_copy(layer, face, distance):
        return pltpu.make_async_remote_copy(
            src_ref=ret_tx.at[layer, face],
            dst_ref=ret_rx.at[layer, face],
            send_sem=r_send.at[layer, face],
            recv_sem=r_recv.at[layer, face],
            device_id=(ahead(distance),),
            device_id_type=MESH,
        )

    def stat_copy(layer, kind, step):
        target, send, recv, partner = (
            (st_a, a_send, a_recv, partner_a),
            (st_b, b_send, b_recv, partner_b),
        )[kind]
        return pltpu.make_async_remote_copy(
            src_ref=st_tx.at[layer, kind],
            dst_ref=target.at[layer, step - 1],
            send_sem=send.at[layer, step - 1],
            recv_sem=recv.at[layer, step - 1],
            device_id=(partner(step),),
            device_id_type=MESH,
        )

    barrier = pltpu.get_barrier_semaphore()
    greeted = [ahead(d) for d in offsets]
    greeted += [partner_a(d) for d in range(1, 8)]
    greeted += [partner_b(d) for d in range(1, n_high)]
    for device in greeted:
        pl.semaphore_signal(barrier, inc=1, device_id=(device,), device_id_type=MESH)

    @pl.loop(0, PAIRS * blocks)
    def _(step):
        in_copy(lax.div(step, blocks), lax.rem(step, blocks)).start()

    @pl.loop(0, nodes // ROWS)
    def _(step):
        rows = pl.ds(step * ROWS, ROWS)
        hb[rows, :] = node_ref[rows, :]
        rowsrc[rows, :] = node_ref[rows, :].astype(F32)

    def gather_rows():
        for face in range(FACES):

            @pl.loop(0, H // 16)
            def _(step):
                for lane in range(16):
                    slot = step * 16 + lane
                    row = rowsrc[pl.ds(send_smem[0, face, slot], 1), :]
                    stage[pl.ds(face * H + slot, 1), :] = row

    gather_rows()
    for face in range(FACES):
        tx0[face] = stage[face * H : (face + 1) * H, :].astype(BF16)
    pl.semaphore_wait(barrier, len(greeted))
    for face in range(FACES):
        halo_copy(0, face).start()

    for layer in range(LAYERS):
        for part in range(3):
            block = ew1[layer, part * T : (part + 1) * T, :].astype(F32)
            w_t[layer, part] = block.T.astype(BF16)
        second = ew2[layer].astype(F32)
        second = second - jnp.mean(second, axis=1, keepdims=True)
        w_t[layer, 3] = second.T.astype(BF16)
        cols[layer, 0] = columns(eb1[layer : layer + 1, :])
        cols[layer, 1] = columns(eg[layer : layer + 1, :])
        cols[layer, 2] = columns(es[layer : layer + 1, :])

    def own_tables(layer, pair_of_groups, latents):
        for part in range(2):
            both = dot_t(w_t[layer, 1 + part], latents).astype(BF16)
            for half in range(2):
                tab[2 * pair_of_groups + half, :, part * T : (part + 1) * T] = both[
                    :, half * T : (half + 1) * T
                ]

    @pl.loop(0, groups // 2)
    def _(step):
        own_tables(0, step, hb[pl.ds(step * 2 * T, 2 * T), :])

    def stage_one(layer, pair, block):
        face_base = (
            nodes
            + (pair * 2 + lax.broadcasted_iota(jnp.int32, (1, 2 * T), 1) // T) * H
        )
        first, far_s, far_r = [], [], []
        for gg in range(GB):
            group = block * GB + gg
            at = pl.multiple_of((group * FACES + pair * 2) * T, T)
            s = ends_ref[0:1, pl.ds(at, 2 * T)]
            r = ends_ref[1:2, pl.ds(at, 2 * T)]
            mine = owned_ref[0:1, pl.ds(at, 2 * T)]
            r = jnp.where(mine > 0, r, -16384)
            near_s = hot(s - group * T, T)
            near_r = hot(r - group * T, T)
            far_s.append(hot(s - face_base, H))
            far_r.append(hot(r - face_base, H))
            ohr[gg] = near_r
            ohh[gg] = far_r[-1]
            got = dot(tab[group], jnp.concatenate([near_s, near_r], axis=0))
            if layer == 0:
                edges = a_buf[group, pl.ds(pair * 2, 2)].reshape(2 * T, T)
                got = got + dot_t(w_t[layer, 0], edges)
            else:
                got = got + dot(w_t[layer, 0], b_buf[group, pair])
            first.append(got)
        bias = cols[layer, 0]
        for face in range(2):
            lanes = slice(face * T, (face + 1) * T)
            for two in range(GB // 2):
                near = (2 * two, 2 * two + 1)
                rhs = jnp.concatenate(
                    [
                        jnp.concatenate([far_s[gg][:, lanes] for gg in near], axis=1),
                        jnp.concatenate([far_r[gg][:, lanes] for gg in near], axis=1),
                    ],
                    axis=0,
                )
                far = dot(htab[face], rhs)
                for half, gg in enumerate(near):
                    before = (
                        first[gg][:, lanes] + far[:, half * T : (half + 1) * T] + bias
                    )
                    hid[gg, :, lanes] = jnp.maximum(before, 0.0).astype(BF16)

    def stage_two(layer, pair, block):
        gain = jnp.concatenate([cols[layer, 1]] * 2, axis=1)
        shift = jnp.concatenate([cols[layer, 2]] * 2, axis=1)
        news = []
        for gg in range(GB):
            group = block * GB + gg
            at = pl.multiple_of((group * FACES + pair * 2) * T, T)
            mine = owned_ref[0:1, pl.ds(at, 2 * T)].astype(F32)
            mixed = dot(w_t[layer, 3], hid[gg])
            spread = jnp.mean(mixed * mixed, axis=0, keepdims=True)
            scale = lax.rsqrt(spread + 1e-05) * mine
            if layer == 0:
                old = a_buf[group, pl.ds(pair * 2, 2)].reshape(2 * T, T).T.astype(F32)
            else:
                old = b_buf[group, pair].astype(F32)
            new = (old + (mixed * scale) * gain + shift * mine).astype(BF16)
            if layer == 0:
                b_buf[group, pair] = new
            else:
                a_buf[group, pl.ds(pair * 2, 2)] = new.T.reshape(2, T, T)
            news.append(new)
            rows = pl.ds(group * T, T)
            agg[rows, :] += dot_t(ohr[gg], new)
        for face in range(2):
            lanes = slice(face * T, (face + 1) * T)
            total = None
            for two in range(GB // 2):
                near = (2 * two, 2 * two + 1)
                part = dot_t(
                    jnp.concatenate([ohh[gg][:, lanes] for gg in near], axis=1),
                    jnp.concatenate([news[gg][:, lanes] for gg in near], axis=1),
                )
                total = part if total is None else total + part
            hsum[face] += total

    def edge_layer(layer, norm):
        @pl.loop(0, nodes // ROWS)
        def _(step):
            agg[pl.ds(step * ROWS, ROWS), :] = jnp.zeros((ROWS, T), F32)

        for pair in range(PAIRS):
            for face in range(2):
                which = 2 * pair + face
                halo_copy(layer, which).wait_recv()
                if layer == 0:
                    rows = rx0[which]
                else:
                    mu, mult, shift = norm
                    update = rx1[which, 0:H, :].astype(F32)
                    update = update + rx1[which, H : H + 1, :].astype(F32)
                    rows = rx0[which].astype(F32) + (update - mu) * mult + shift
                    rows = rows.astype(BF16)
                for part in range(2):
                    htab[face, :, part * H : (part + 1) * H] = dot_t(
                        w_t[layer, 1 + part], rows
                    ).astype(BF16)
            hsum[...] = jnp.zeros_like(hsum)
            if layer == 0:
                in_copy(pair, 0).wait()
            stage_one(layer, pair, 0)

            @pl.loop(1, blocks)
            def _(block):
                if layer == 0:
                    in_copy(pair, block).wait()
                stage_two(layer, pair, block - 1)
                stage_one(layer, pair, block)
                if layer == 1:
                    out_copy(pair, block - 1).start()

            stage_two(layer, pair, blocks - 1)
            if layer == 1:
                out_copy(pair, blocks - 1).start()
            for face in range(2):
                which = 2 * pair + face
                ret_tx[layer, which] = hsum[face].astype(BF16)
            for face in range(2):
                which = 2 * pair + face
                return_copy(layer, which, n_dev - offsets[which]).start()

    def node_layer(layer):
        for face in range(FACES):
            return_copy(layer, face, n_dev - offsets[face]).wait_recv()

        def step_of(step, carry):
            sums, squares = carry
            rows = pl.ds(step * ROWS, ROWS)
            extra = None
            for face in range(FACES):
                picks = hot(send_ref[0, face : face + 1, :] - step * ROWS, ROWS)
                part = dot(picks, ret_rx[layer, face])
                extra = part if extra is None else extra + part
            total = (agg[rows, :] + extra).astype(BF16)
            joined = jnp.concatenate([hb[rows, :], total], axis=1)
            hidden = dot(joined, nw1[layer]) + nb1[layer : layer + 1, :]
            hidden = jnp.maximum(hidden, 0.0).astype(BF16)
            update = dot(hidden, nw2[layer])
            rowsrc[rows, :] = update
            cut = update.reshape(ROWS // 8, 8, T)
            return sums + jnp.sum(cut, axis=0), squares + jnp.sum(cut * cut, axis=0)

        zero = jnp.zeros((8, T), F32)
        sums, squares = lax.fori_loop(0, nodes // ROWS, step_of, (zero, zero))
        sums = jnp.sum(sums, axis=0, keepdims=True)
        squares = jnp.sum(squares, axis=0, keepdims=True)
        first = lax.broadcasted_iota(jnp.int32, (8, T), 0) == 0
        return sums, jnp.where(first, sums, squares)

    def reduce_start(layer, mine):
        st_tx[layer, 0] = mine
        for step in range(1, 8):
            stat_copy(layer, 0, step).start()

    def reduce_finish(layer, mine):
        for step in range(1, 8):
            stat_copy(layer, 0, step).wait_recv()
        for step in range(1, 8):
            mine = mine + st_a[layer, step - 1]
        st_tx[layer, 1] = mine
        for step in range(1, n_high):
            stat_copy(layer, 1, step).start()
        for step in range(1, n_high):
            stat_copy(layer, 1, step).wait_recv()
        for step in range(1, n_high):
            mine = mine + st_b[layer, step - 1]
        count = nodes * n_dev
        mu = mine[0:1, :] / count
        var = jnp.maximum(mine[1:2, :] / count - mu * mu, 0.0)
        mult = ng[layer : layer + 1, :] * lax.rsqrt(var + 1e-05)
        return mu, mult, ns[layer : layer + 1, :]

    edge_layer(0, None)
    sums, mine = node_layer(0)
    reduce_start(0, mine)
    gather_rows()
    ref = (sums / nodes).astype(BF16)
    ref_wide = ref.astype(F32)
    for face in range(FACES):
        delta = stage[face * H : (face + 1) * H, :] - ref_wide
        tx1[face, 0:H, :] = delta.astype(BF16)
        tx1[face, H : H + REF, :] = jnp.broadcast_to(ref_wide, (REF, T)).astype(BF16)
    for face in range(FACES):
        halo_copy(1, face).start()
    mu, mult, shift = reduce_finish(0, mine)

    @pl.loop(0, groups // 2)
    def _(step):
        rows = pl.ds(step * 2 * T, 2 * T)
        new = hb[rows, :].astype(F32) + (rowsrc[rows, :] - mu) * mult + shift
        new = new.astype(BF16)
        hb[rows, :] = new
        own_tables(1, step, new)

    edge_layer(1, (mu, mult, shift))
    _, mine = node_layer(1)
    reduce_start(1, mine)
    mu, mult, shift = reduce_finish(1, mine)

    @pl.loop(0, nodes // ROWS)
    def _(step):
        rows = pl.ds(step * ROWS, ROWS)
        new = hb[rows, :].astype(F32) + (rowsrc[rows, :] - mu) * mult + shift
        node_out[rows, :] = new.astype(BF16)

    @pl.loop(0, PAIRS * blocks)
    def _(step):
        out_copy(lax.div(step, blocks), lax.rem(step, blocks)).wait()

    for layer in range(LAYERS):
        for face in range(FACES):
            halo_copy(layer, face).wait_send()
            return_copy(layer, face, n_dev - offsets[face]).wait_send()
        for step in range(1, 8):
            stat_copy(layer, 0, step).wait_send()
        for step in range(1, n_high):
            stat_copy(layer, 1, step).wait_send()


def per_device(
    n_dev,
    node_latent,
    edge_latent,
    edge_ends,
    edge_owned,
    send_index,
    *weights,
):
    nodes = node_latent.shape[0]
    groups = nodes // T
    slots = edge_latent.shape[0]
    vmem = pl.BlockSpec(memory_space=pltpu.VMEM)
    smem = pl.BlockSpec(memory_space=pltpu.SMEM)
    anywhere = pl.BlockSpec(memory_space=pl.ANY)
    n_copies = PAIRS * (groups // GB)
    n_high = n_dev // 8
    dma = pltpu.SemaphoreType.DMA
    node_out, edge_out = pl.pallas_call(
        functools.partial(kernel, n_dev, groups),
        out_shape=(
            jax.ShapeDtypeStruct((nodes, T), BF16),
            jax.ShapeDtypeStruct((groups, FACES, T, T), BF16),
        ),
        in_specs=[vmem, anywhere, vmem, vmem, smem, vmem] + [vmem] * len(weights),
        out_specs=(vmem, anywhere),
        scratch_shapes=[
            pltpu.VMEM((groups, FACES, T, T), BF16),
            pltpu.VMEM((groups, PAIRS, T, 2 * T), BF16),
            pltpu.VMEM((nodes, T), BF16),
            pltpu.VMEM((nodes, T), F32),
            pltpu.VMEM((nodes, T), F32),
            pltpu.VMEM((groups, T, 2 * T), BF16),
            pltpu.VMEM((2, T, 2 * H), BF16),
            pltpu.VMEM((GB, T, 2 * T), BF16),
            pltpu.VMEM((GB, T, 2 * T), BF16),
            pltpu.VMEM((GB, H, 2 * T), BF16),
            pltpu.VMEM((2, H, T), F32),
            pltpu.VMEM((FACES * H, T), F32),
            pltpu.VMEM((FACES, H, T), BF16),
            pltpu.VMEM((FACES, H + REF, T), BF16),
            pltpu.VMEM((FACES, H, T), BF16),
            pltpu.VMEM((FACES, H + REF, T), BF16),
            pltpu.VMEM((LAYERS, FACES, H, T), BF16),
            pltpu.VMEM((LAYERS, FACES, H, T), BF16),
            pltpu.VMEM((LAYERS, 4, T, T), BF16),
            pltpu.VMEM((LAYERS, 3, T, T), F32),
            pltpu.VMEM((LAYERS, 2, 8, T), F32),
            pltpu.VMEM((LAYERS, 7, 8, T), F32),
            pltpu.VMEM((LAYERS, n_high - 1, 8, T), F32),
            dma((n_copies,)),
            dma((n_copies,)),
            dma((LAYERS, FACES)),
            dma((LAYERS, FACES)),
            dma((LAYERS, FACES)),
            dma((LAYERS, FACES)),
            dma((LAYERS, 7)),
            dma((LAYERS, 7)),
            dma((LAYERS, n_high - 1)),
            dma((LAYERS, n_high - 1)),
        ],
        compiler_params=pltpu.CompilerParams(
            collective_id=0, has_side_effects=True, vmem_limit_bytes=60 * 1024 * 1024
        ),
    )(
        node_latent,
        edge_latent.reshape(groups, FACES, T, T),
        edge_ends,
        edge_owned.reshape(1, slots),
        send_index,
        send_index,
        *weights,
    )
    return node_out, edge_out.reshape(slots, T)


def solution(mesh):
    return jax.shard_map(
        functools.partial(per_device, mesh.shape["blk"]),
        mesh=mesh,
        in_specs=(
            P("blk", None),
            P("blk", None),
            P(None, "blk"),
            P("blk"),
            P("blk", None, None),
        )
        + (P(),) * 10,
        out_specs=(P("blk", None), P("blk", None)),
        check_vma=False,
    )
```

time: 381 us -> 126 us (0.33); the launches traced: 375 us -> 125 us
  Pallas kernels: 0 us -> 115 us
  matrix products: 106 us -> 0 us
  other arithmetic: 97.5 us -> 0 us
  blocking collectives: 67.3 us -> 0 us
  starting transfers between devices: 61 us -> 0 us
  waiting for transfers between devices: 29.6 us -> 0 us
    pallas_call x0 -> x1, Pallas kernels: none -> 115 us  [per_device(): pl.pallas_call(functools.partial(kernel, n_dev, groups), out_shape=(jax.S...]
    dot_general x16 -> x0, matrix products: 106 us -> none  [the longest x4 34.1 us: select_rows(): jnp.einsum('bkeh,khc->bkec', halo_hot, halo_view, preferred_element_type=...]
    psum x8 -> x0, blocking collectives: 67.3 us -> none  [over_axes(): return functools.reduce(lax.psum, axes, shard)]
    ppermute x24 -> x0, starting transfers between devices: 61 us -> none  [passed_along(): return lax.ppermute(block, axis, route)]
    convert_element_type x7 -> x0, other arithmetic: 53.8 us -> none  [the longest x2 44.4 us: per_device(): message = (owned * edges_new.astype(jnp.float32)).astype(jnp.bfloat16).re...]
    ppermute x24 -> x0, waiting for transfers between devices: 29.6 us -> none  [passed_along(): return lax.ppermute(block, axis, route)]
    scatter-add x2 -> x0, other arithmetic: 21.7 us -> none  [per_device(): node_sums = own_sums.at[flat_faces].add(jnp.concatenate(returned, axis=0))]
    reduce_sum x2 -> x0, other arithmetic: 21 us -> none  [row_norm(): spread = jnp.mean(centre * centre, axis=1, keepdims=True)]
  transfers between devices with their start and end apart: 24 -> 0, of which waited for: 5 -> 0; matrix products, arithmetic and copies ran while one was open for 10% -> 0% of each run, Pallas kernels for 0% -> 0%
where the time goes in v1:
time: 126 us; the launch traced here: 125 us
  Pallas kernels  115 us (91%)
  local copies, waits for them, and re-layouts  9.97 us (8%)
    pallas_call x1, Pallas kernels, per_device(): pl.pallas_call(functools.partial(kernel, n_dev, groups), out_shape=(jax.S...  115 us
    unnamed x3, local copies, waits for them, and re-layouts  9.97 us

profile of v1, /device:TPU:1, one launch (start us, length us, event | category | flops | bytes accessed | tf_op | source)
XLA Modules:
  0.0 125.5 jit_solution(14765965880177102344)
XLA Ops:
  0.6 1.3 %copy.17.send_smem.send_ref = s32[1,6,256]{2,1,0:T(8,128)} copy(s32[1,6,256]{2,0,1:T(1,128)} %param.19) | data formatting | bytes 12288 | tf_op args[4]
  1.9 114.9 %shard_map.158 = (bf16[4096,128]{1,0:T(8,128)(2,1)}, bf16[32,6,128,128]{3,2,1,0:T(8,128)(2,1)}) custom-call(bf16[4096,128]{1,0:T(8,128)(2,1)} %node_ref.1, bf16[32,6,128,128]{3,2,1,0:T(8,128)(2,1)} %bitcast.4, s32[2,24576]{1,0:T(2,128)} %ends_ref.1, s32[1,24576]{1,0:T(1,128)} %bitcast.5, s32[1,6,256]{2,1,0:T(8,128)} %copy.17.send_smem.send_ref, ...), custom_call_target="tpu_custom_call" | custom-call | tf_op jit(solution)/shard_map/pallas_call | solution.py:459
  116.8 2.3 %copy.21 = bf16[4096,128]{1,0:T(8,128)(2,1)} copy(bf16[4096,128]{1,0:T(8,128)(2,1)} %get-tuple-element.8) | data formatting | bytes 2097152
  119.1 6.4 %copy.22 = bf16[24576,128]{1,0:T(8,128)(2,1)} copy(bf16[24576,128]{1,0:T(8,128)(2,1)} %bitcast.3) | data formatting | bytes 12582912

commit v2 on v1

--- a/solution.py
+++ b/solution.py
@@ -13,10 +13,13 @@
 LAYERS = 2
 FACES = 6
 PAIRS = 3
+ORDER = (2, 1, 0)
 T = 128
 H = 256
+SEQUENCE = tuple(2 * pair + face for pair in ORDER for face in range(2))
 GB = 4
 REF = 16
+PART, PARTS = 256, 4
 ROWS = 512
 
 
@@ -69,8 +72,8 @@
     tab,
     htab,
     hid,
-    ohr,
-    ohh,
+    near_hot,
+    far_hot,
     hsum,
     stage,
     tx0,
@@ -176,20 +179,17 @@
         rowsrc[rows, :] = node_ref[rows, :].astype(F32)
 
     def gather_rows():
-        for face in range(FACES):
-
-            @pl.loop(0, H // 16)
-            def _(step):
-                for lane in range(16):
-                    slot = step * 16 + lane
-                    row = rowsrc[pl.ds(send_smem[0, face, slot], 1), :]
-                    stage[pl.ds(face * H + slot, 1), :] = row
+        @pl.loop(0, FACES)
+        def _(face):
+            for slot in range(H):
+                row = rowsrc[pl.ds(send_smem[face, 0, slot], 1), :]
+                stage[pl.ds(face * H + slot, 1), :] = row
 
     gather_rows()
     for face in range(FACES):
         tx0[face] = stage[face * H : (face + 1) * H, :].astype(BF16)
     pl.semaphore_wait(barrier, len(greeted))
-    for face in range(FACES):
+    for face in SEQUENCE:
         halo_copy(0, face).start()
 
     for layer in range(LAYERS):
@@ -203,72 +203,85 @@
         cols[layer, 1] = columns(eg[layer : layer + 1, :])
         cols[layer, 2] = columns(es[layer : layer + 1, :])
 
+    def both_ways(layer):
+        return w_t[layer, 1:3].reshape(2 * T, T)
+
     def own_tables(layer, pair_of_groups, latents):
-        for part in range(2):
-            both = dot_t(w_t[layer, 1 + part], latents).astype(BF16)
-            for half in range(2):
+        both = dot_t(both_ways(layer), latents).astype(BF16)
+        for half in range(2):
+            for part in range(2):
                 tab[2 * pair_of_groups + half, :, part * T : (part + 1) * T] = both[
-                    :, half * T : (half + 1) * T
+                    part * T : (part + 1) * T, half * T : (half + 1) * T
                 ]
 
-    @pl.loop(0, groups // 2)
+    @pl.loop(0, groups // 2, unroll=4)
     def _(step):
         own_tables(0, step, hb[pl.ds(step * 2 * T, 2 * T), :])
 
-    def stage_one(layer, pair, block):
-        face_base = (
-            nodes
-            + (pair * 2 + lax.broadcasted_iota(jnp.int32, (1, 2 * T), 1) // T) * H
-        )
-        first, far_s, far_r = [], [], []
+    def ends_of(pair, group):
+        at = pl.multiple_of((group * FACES + pair * 2) * T, T)
+        lanes = pl.ds(at, 2 * T)
+        return ends_ref[0:1, lanes], ends_ref[1:2, lanes], owned_ref[0:1, lanes]
+
+    @pl.loop(0, blocks)
+    def _(block):
+        for pair in ORDER:
+            which = lax.broadcasted_iota(jnp.int32, (1, 2 * T), 1) // T
+            face_base = nodes + (pair * 2 + which) * H
+            for gg in range(GB):
+                group = block * GB + gg
+                s, r, mine = ends_of(pair, group)
+                far = hot(jnp.where(r >= nodes, r, s) - face_base, H)
+                for face in range(2):
+                    far_hot[2 * pair + face, block, :, gg * T : (gg + 1) * T] = far[
+                        :, face * T : (face + 1) * T
+                    ]
+                near_hot[group, pair, 0:T, :] = hot(s - group * T, T)
+                r = jnp.where(mine > 0, r, -16384)
+                near_hot[group, pair, T : 2 * T, :] = hot(r - group * T, T)
+
+    def gather(layer, pair, block):
+        first, far = [], []
         for gg in range(GB):
             group = block * GB + gg
-            at = pl.multiple_of((group * FACES + pair * 2) * T, T)
-            s = ends_ref[0:1, pl.ds(at, 2 * T)]
-            r = ends_ref[1:2, pl.ds(at, 2 * T)]
-            mine = owned_ref[0:1, pl.ds(at, 2 * T)]
-            r = jnp.where(mine > 0, r, -16384)
-            near_s = hot(s - group * T, T)
-            near_r = hot(r - group * T, T)
-            far_s.append(hot(s - face_base, H))
-            far_r.append(hot(r - face_base, H))
-            ohr[gg] = near_r
-            ohh[gg] = far_r[-1]
-            got = dot(tab[group], jnp.concatenate([near_s, near_r], axis=0))
+            got = dot(tab[group], near_hot[group, pair])
             if layer == 0:
                 edges = a_buf[group, pl.ds(pair * 2, 2)].reshape(2 * T, T)
                 got = got + dot_t(w_t[layer, 0], edges)
             else:
                 got = got + dot(w_t[layer, 0], b_buf[group, pair])
             first.append(got)
+        for face in range(2):
+            for two in range(GB // 2):
+                at = slice(two * 2 * T, (two + 1) * 2 * T)
+                far.append(dot(htab[2 * pair + face], far_hot[2 * pair + face, block, :, at]))
+        return first, far
+
+    def hide(layer, pair, block, gathered):
+        first, far = gathered
         bias = cols[layer, 0]
         for face in range(2):
             lanes = slice(face * T, (face + 1) * T)
-            for two in range(GB // 2):
-                near = (2 * two, 2 * two + 1)
-                rhs = jnp.concatenate(
-                    [
-                        jnp.concatenate([far_s[gg][:, lanes] for gg in near], axis=1),
-                        jnp.concatenate([far_r[gg][:, lanes] for gg in near], axis=1),
-                    ],
-                    axis=0,
-                )
-                far = dot(htab[face], rhs)
-                for half, gg in enumerate(near):
-                    before = (
-                        first[gg][:, lanes] + far[:, half * T : (half + 1) * T] + bias
-                    )
-                    hid[gg, :, lanes] = jnp.maximum(before, 0.0).astype(BF16)
-
-    def stage_two(layer, pair, block):
+            for gg in range(GB):
+                remote = ends_of(pair, block * GB + gg)[0][:, lanes] >= nodes
+                mask = jnp.broadcast_to(remote, (T, T))
+                both = far[face * (GB // 2) + gg // 2]
+                side = slice(gg % 2 * T, (gg % 2 + 1) * T)
+                add = jnp.where(mask, both[0:T, side], both[T : 2 * T, side])
+                before = first[gg][:, lanes] + bias + add
+                hid[gg, :, lanes] = jnp.maximum(before, 0.0).astype(BF16)
+
+    def mix(layer):
+        return [dot(w_t[layer, 3], hid[gg]) for gg in range(GB)]
+
+    def renew(layer, pair, block, mixes):
         gain = jnp.concatenate([cols[layer, 1]] * 2, axis=1)
         shift = jnp.concatenate([cols[layer, 2]] * 2, axis=1)
         news = []
         for gg in range(GB):
             group = block * GB + gg
-            at = pl.multiple_of((group * FACES + pair * 2) * T, T)
-            mine = owned_ref[0:1, pl.ds(at, 2 * T)].astype(F32)
-            mixed = dot(w_t[layer, 3], hid[gg])
+            mixed = mixes[gg]
+            mine = ends_of(pair, group)[2].astype(F32)
             spread = jnp.mean(mixed * mixed, axis=0, keepdims=True)
             scale = lax.rsqrt(spread + 1e-05) * mine
             if layer == 0:
@@ -281,29 +294,38 @@
             else:
                 a_buf[group, pl.ds(pair * 2, 2)] = new.T.reshape(2, T, T)
             news.append(new)
+        return news
+
+    def scatter(pair, block, news):
+        sent = []
+        for gg in range(GB):
+            group = block * GB + gg
             rows = pl.ds(group * T, T)
-            agg[rows, :] += dot_t(ohr[gg], new)
+            agg[rows, :] += dot_t(near_hot[group, pair, T : 2 * T, :], news[gg])
+            _, r, mine = ends_of(pair, group)
+            leaves = jnp.where((r >= nodes) & (mine > 0), 1.0, 0.0)
+            wide = jnp.broadcast_to(leaves, (16, 2 * T)).astype(BF16)
+            kept = news[gg].reshape(T // 16, 16, 2 * T) * wide[None]
+            sent.append(kept.reshape(T, 2 * T))
         for face in range(2):
             lanes = slice(face * T, (face + 1) * T)
-            total = None
-            for two in range(GB // 2):
-                near = (2 * two, 2 * two + 1)
-                part = dot_t(
-                    jnp.concatenate([ohh[gg][:, lanes] for gg in near], axis=1),
-                    jnp.concatenate([news[gg][:, lanes] for gg in near], axis=1),
-                )
-                total = part if total is None else total + part
-            hsum[face] += total
+            message = jnp.concatenate([part[:, lanes] for part in sent], axis=1)
+            hsum[2 * pair + face] += dot_t(far_hot[2 * pair + face, block], message)
 
     def edge_layer(layer, norm):
         @pl.loop(0, nodes // ROWS)
         def _(step):
             agg[pl.ds(step * ROWS, ROWS), :] = jnp.zeros((ROWS, T), F32)
 
-        for pair in range(PAIRS):
-            for face in range(2):
-                which = 2 * pair + face
+        hsum[...] = jnp.zeros_like(hsum)
+
+        def halo_tables(pair):
+            faces = (2 * pair, 2 * pair + 1)
+            for which in faces:
                 halo_copy(layer, which).wait_recv()
+            if layer == 0:
+                in_copy(pair, 0).wait()
+            for which in faces:
                 if layer == 0:
                     rows = rx0[which]
                 else:
@@ -312,57 +334,89 @@
                     update = update + rx1[which, H : H + 1, :].astype(F32)
                     rows = rx0[which].astype(F32) + (update - mu) * mult + shift
                     rows = rows.astype(BF16)
-                for part in range(2):
-                    htab[face, :, part * H : (part + 1) * H] = dot_t(
-                        w_t[layer, 1 + part], rows
-                    ).astype(BF16)
-            hsum[...] = jnp.zeros_like(hsum)
+                htab[which] = dot_t(both_ways(layer), rows).astype(BF16)
+
+        def turn(pair, block, pair_next, block_next):
+            mixes = mix(layer)
+            gathered = gather(layer, pair_next, block_next)
+            news = renew(layer, pair, block, mixes)
+            scatter(pair, block, news)
+            hide(layer, pair_next, block_next, gathered)
+
+        halo_tables(ORDER[0])
+        hide(layer, ORDER[0], 0, gather(layer, ORDER[0], 0))
+        for place, pair in enumerate(ORDER):
+
+            @pl.loop(0, blocks // 2 - 1)
+            def _(double):
+                block = 2 * double
+                if layer == 0:
+                    in_copy(pair, block + 1).wait()
+                    in_copy(pair, block + 2).wait()
+                turn(pair, block, pair, block + 1)
+                turn(pair, block + 1, pair, block + 2)
+                if layer == 1:
+                    out_copy(pair, block).start()
+                    out_copy(pair, block + 1).start()
+
+            last = blocks - 1
             if layer == 0:
-                in_copy(pair, 0).wait()
-            stage_one(layer, pair, 0)
-
-            @pl.loop(1, blocks)
-            def _(block):
-                if layer == 0:
-                    in_copy(pair, block).wait()
-                stage_two(layer, pair, block - 1)
-                stage_one(layer, pair, block)
-                if layer == 1:
-                    out_copy(pair, block - 1).start()
-
-            stage_two(layer, pair, blocks - 1)
+                in_copy(pair, last).wait()
+            if place + 1 < PAIRS:
+                halo_tables(ORDER[place + 1])
+                turn(pair, last - 1, pair, last)
+                turn(pair, last, ORDER[place + 1], 0)
+            else:
+                turn(pair, last - 1, pair, last)
+                scatter(pair, last, renew(layer, pair, last, mix(layer)))
             if layer == 1:
-                out_copy(pair, blocks - 1).start()
-            for face in range(2):
-                which = 2 * pair + face
-                ret_tx[layer, which] = hsum[face].astype(BF16)
-            for face in range(2):
-                which = 2 * pair + face
+                out_copy(pair, last - 1).start()
+                out_copy(pair, last).start()
+            for which in (2 * pair, 2 * pair + 1):
+                ret_tx[layer, which] = hsum[which].astype(BF16)
+            for which in (2 * pair, 2 * pair + 1):
                 return_copy(layer, which, n_dev - offsets[which]).start()
 
+    def returned(layer, faces, start, rows):
+        extra = agg[pl.ds(start, rows), :]
+        for face in faces:
+            picks = hot(send_ref[face] - start, rows)
+            extra = extra + dot(picks, ret_rx[layer, face])
+        return extra
+
     def node_layer(layer):
-        for face in range(FACES):
+        early, late = SEQUENCE[:4], SEQUENCE[4:]
+        for face in early:
+            return_copy(layer, face, n_dev - offsets[face]).wait_recv()
+
+        @pl.loop(0, nodes // ROWS, unroll=2)
+        def _(step):
+            agg[pl.ds(step * ROWS, ROWS), :] = returned(layer, early, step * ROWS, ROWS)
+
+        for face in late:
             return_copy(layer, face, n_dev - offsets[face]).wait_recv()
 
         def step_of(step, carry):
             sums, squares = carry
-            rows = pl.ds(step * ROWS, ROWS)
-            extra = None
-            for face in range(FACES):
-                picks = hot(send_ref[0, face : face + 1, :] - step * ROWS, ROWS)
-                part = dot(picks, ret_rx[layer, face])
-                extra = part if extra is None else extra + part
-            total = (agg[rows, :] + extra).astype(BF16)
-            joined = jnp.concatenate([hb[rows, :], total], axis=1)
-            hidden = dot(joined, nw1[layer]) + nb1[layer : layer + 1, :]
-            hidden = jnp.maximum(hidden, 0.0).astype(BF16)
-            update = dot(hidden, nw2[layer])
-            rowsrc[rows, :] = update
-            cut = update.reshape(ROWS // 8, 8, T)
-            return sums + jnp.sum(cut, axis=0), squares + jnp.sum(cut * cut, axis=0)
+            starts = [step * (PARTS * PART) + part * PART for part in range(PARTS)]
+            totals = [returned(layer, late, at, PART).astype(BF16) for at in starts]
+            hiddens = []
+            for at, total in zip(starts, totals):
+                joined = jnp.concatenate([hb[pl.ds(at, PART), :], total], axis=1)
+                hidden = dot(joined, nw1[layer]) + nb1[layer : layer + 1, :]
+                hiddens.append(jnp.maximum(hidden, 0.0).astype(BF16))
+            for at, hidden in zip(starts, hiddens):
+                update = dot(hidden, nw2[layer])
+                rowsrc[pl.ds(at, PART), :] = update
+                cut = update.reshape(PART // 8, 8, T)
+                sums = sums + jnp.sum(cut, axis=0)
+                squares = squares + jnp.sum(cut * cut, axis=0)
+            return sums, squares
 
         zero = jnp.zeros((8, T), F32)
-        sums, squares = lax.fori_loop(0, nodes // ROWS, step_of, (zero, zero))
+        sums, squares = lax.fori_loop(
+            0, nodes // (PARTS * PART), step_of, (zero, zero)
+        )
         sums = jnp.sum(sums, axis=0, keepdims=True)
         squares = jnp.sum(squares, axis=0, keepdims=True)
         first = lax.broadcasted_iota(jnp.int32, (8, T), 0) == 0
@@ -401,11 +455,11 @@
         delta = stage[face * H : (face + 1) * H, :] - ref_wide
         tx1[face, 0:H, :] = delta.astype(BF16)
         tx1[face, H : H + REF, :] = jnp.broadcast_to(ref_wide, (REF, T)).astype(BF16)
-    for face in range(FACES):
+    for face in SEQUENCE:
         halo_copy(1, face).start()
     mu, mult, shift = reduce_finish(0, mine)
 
-    @pl.loop(0, groups // 2)
+    @pl.loop(0, groups // 2, unroll=4)
     def _(step):
         rows = pl.ds(step * 2 * T, 2 * T)
         new = hb[rows, :].astype(F32) + (rowsrc[rows, :] - mu) * mult + shift
@@ -471,11 +525,11 @@
             pltpu.VMEM((nodes, T), F32),
             pltpu.VMEM((nodes, T), F32),
             pltpu.VMEM((groups, T, 2 * T), BF16),
-            pltpu.VMEM((2, T, 2 * H), BF16),
+            pltpu.VMEM((FACES, 2 * T, H), BF16),
             pltpu.VMEM((GB, T, 2 * T), BF16),
-            pltpu.VMEM((GB, T, 2 * T), BF16),
-            pltpu.VMEM((GB, H, 2 * T), BF16),
-            pltpu.VMEM((2, H, T), F32),
+            pltpu.VMEM((groups, PAIRS, 2 * T, 2 * T), BF16),
+            pltpu.VMEM((FACES, groups // GB, H, GB * T), BF16),
+            pltpu.VMEM((FACES, H, T), F32),
             pltpu.VMEM((FACES * H, T), F32),
             pltpu.VMEM((FACES, H, T), BF16),
             pltpu.VMEM((FACES, H + REF, T), BF16),
@@ -500,15 +554,15 @@
             dma((LAYERS, n_high - 1)),
         ],
         compiler_params=pltpu.CompilerParams(
-            collective_id=0, has_side_effects=True, vmem_limit_bytes=60 * 1024 * 1024
+            collective_id=0, has_side_effects=True, vmem_limit_bytes=56 * 1024 * 1024
         ),
     )(
         node_latent,
         edge_latent.reshape(groups, FACES, T, T),
         edge_ends,
         edge_owned.reshape(1, slots),
-        send_index,
-        send_index,
+        send_index.reshape(FACES, 1, H),
+        send_index.reshape(FACES, 1, H),
         *weights,
     )
     return node_out, edge_out.reshape(slots, T)

time: 126 us -> 96.8 us (0.77)
  Pallas kernels: 115 us -> 87.3 us
  local copies, waits for them, and re-layouts: 9.97 us -> 8.68 us
    pallas_call x1, Pallas kernels: 115 us -> 87.3 us  [per_device(): pl.pallas_call(functools.partial(kernel, n_dev, groups), out_shape=(jax.S...]
    unnamed x3 -> x2, local copies, waits for them, and re-layouts: 9.97 us -> 8.68 us
where the time goes in v2:
time: 96.8 us; the launch traced here: 96.6 us
  Pallas kernels  87.3 us (90%)
  local copies, waits for them, and re-layouts  8.68 us (9%)
    pallas_call x1, Pallas kernels, per_device(): pl.pallas_call(functools.partial(kernel, n_dev, groups), out_shape=(jax.S...  87.3 us
    unnamed x2, local copies, waits for them, and re-layouts  8.68 us

profile of v2, /device:TPU:1, one launch (start us, length us, event | category | flops | bytes accessed | tf_op | source)
XLA Modules:
  0.0 96.6 jit_solution(1724153059773894695)
XLA Ops:
  0.6 87.3 %shard_map.158 = (bf16[4096,128]{1,0:T(8,128)(2,1)}, bf16[32,6,128,128]{3,2,1,0:T(8,128)(2,1)}) custom-call(bf16[4096,128]{1,0:T(8,128)(2,1)} %node_ref.1, bf16[32,6,128,128]{3,2,1,0:T(8,128)(2,1)} %bitcast.4, s32[2,24576]{1,0:T(2,128)} %ends_ref.1, s32[1,24576]{1,0:T(1,128)} %bitcast.6, s32[6,1,256]{2,1,0:T(1,128)} %bitcast.7, s32[6,1,256]{2,1,0:T(1,128)} %bitcast.8, ...), custom_call_target="tpu_custom_call" | custom-call | tf_op jit(solution)/shard_map/pallas_call | solution.py:513
  87.9 2.3 %copy.19 = bf16[4096,128]{1,0:T(8,128)(2,1)} copy(bf16[4096,128]{1,0:T(8,128)(2,1)} %get-tuple-element.8) | data formatting | bytes 2097152
  90.2 6.4 %copy.20 = bf16[24576,128]{1,0:T(8,128)(2,1)} copy(bf16[24576,128]{1,0:T(8,128)(2,1)} %bitcast.5) | data formatting | bytes 12582912

commit v3 on v2

--- a/solution.py
+++ b/solution.py
@@ -97,6 +97,7 @@
     a_recv,
     b_send,
     b_recv,
+    node_sem,
 ):
     me = lax.axis_index("blk")
     nodes = groups * T
@@ -476,7 +477,10 @@
     def _(step):
         rows = pl.ds(step * ROWS, ROWS)
         new = hb[rows, :].astype(F32) + (rowsrc[rows, :] - mu) * mult + shift
-        node_out[rows, :] = new.astype(BF16)
+        hb[rows, :] = new.astype(BF16)
+
+    node_copy = pltpu.make_async_copy(hb, node_out, node_sem)
+    node_copy.start()
 
     @pl.loop(0, PAIRS * blocks)
     def _(step):
@@ -490,6 +494,8 @@
             stat_copy(layer, 0, step).wait_send()
         for step in range(1, n_high):
             stat_copy(layer, 1, step).wait_send()
+
+    node_copy.wait()
 
 
 def per_device(
@@ -513,11 +519,11 @@
     node_out, edge_out = pl.pallas_call(
         functools.partial(kernel, n_dev, groups),
         out_shape=(
-            jax.ShapeDtypeStruct((nodes, T), BF16),
-            jax.ShapeDtypeStruct((groups, FACES, T, T), BF16),
+            pltpu.VMEM((nodes, T), BF16),
+            pltpu.VMEM((groups, FACES, T, T), BF16),
         ),
         in_specs=[vmem, anywhere, vmem, vmem, smem, vmem] + [vmem] * len(weights),
-        out_specs=(vmem, anywhere),
+        out_specs=(anywhere, anywhere),
         scratch_shapes=[
             pltpu.VMEM((groups, FACES, T, T), BF16),
             pltpu.VMEM((groups, PAIRS, T, 2 * T), BF16),
@@ -552,6 +558,7 @@
             dma((LAYERS, 7)),
             dma((LAYERS, n_high - 1)),
             dma((LAYERS, n_high - 1)),
+            dma,
         ],
         compiler_params=pltpu.CompilerParams(
             collective_id=0, has_side_effects=True, vmem_limit_bytes=56 * 1024 * 1024

time: 96.8 us -> 91.4 us (0.944)
  local copies, waits for them, and re-layouts: 8.68 us -> 3.68 us
    unnamed x2, local copies, waits for them, and re-layouts: 8.68 us -> 3.68 us
where the time goes in v3:
time: 91.4 us; the launch traced here: 91.2 us
  Pallas kernels  86.9 us (95%)
  local copies, waits for them, and re-layouts  3.68 us (4%)
    pallas_call x1, Pallas kernels, per_device(): pl.pallas_call(functools.partial(kernel, n_dev, groups), out_shape=(pltpu...  86.9 us
    unnamed x2, local copies, waits for them, and re-layouts  3.68 us

profile of v3, /device:TPU:1, one launch (start us, length us, event | category | flops | bytes accessed | tf_op | source)
XLA Modules:
  0.0 91.2 jit_solution(13793980898927141970)
XLA Ops:
  0.6 86.9 %shard_map.158 = (bf16[4096,128]{1,0:T(8,128)(2,1)S(1)}, bf16[32,6,128,128]{3,2,1,0:T(8,128)(2,1)S(1)}) custom-call(bf16[4096,128]{1,0:T(8,128)(2,1)} %node_ref.1, bf16[32,6,128,128]{3,2,1,0:T(8,128)(2,1)} %bitcast.5, s32[2,24576]{1,0:T(2,128)} %ends_ref.1, s32[1,24576]{1,0:T(1,128)} %bitcast.6, s32[6,1,256]{2,1,0:T(1,128)} %bitcast.7, ...), custom_call_target="tpu_custom_call" | custom-call | tf_op jit(solution)/shard_map/pallas_call | solution.py:519
  87.5 1.0 %copy.19 = bf16[4096,128]{1,0:T(8,128)(2,1)} copy(bf16[4096,128]{1,0:T(8,128)(2,1)S(1)} %get-tuple-element.6) | data formatting | bytes 2097152
  88.5 2.7 %copy.20 = bf16[24576,128]{1,0:T(8,128)(2,1)} copy(bf16[24576,128]{1,0:T(8,128)(2,1)S(1)} %bitcast.4) | data formatting | bytes 12582912

commit v4 on v3

--- a/solution.py
+++ b/solution.py
@@ -313,13 +313,14 @@
             message = jnp.concatenate([part[:, lanes] for part in sent], axis=1)
             hsum[2 * pair + face] += dot_t(far_hot[2 * pair + face, block], message)
 
-    def edge_layer(layer, norm):
+    def clear():
         @pl.loop(0, nodes // ROWS)
         def _(step):
             agg[pl.ds(step * ROWS, ROWS), :] = jnp.zeros((ROWS, T), F32)
 
         hsum[...] = jnp.zeros_like(hsum)
 
+    def edge_layer(layer, norm):
         def halo_tables(pair):
             faces = (2 * pair, 2 * pair + 1)
             for which in faces:
@@ -420,15 +421,28 @@
         )
         sums = jnp.sum(sums, axis=0, keepdims=True)
         squares = jnp.sum(squares, axis=0, keepdims=True)
-        first = lax.broadcasted_iota(jnp.int32, (8, T), 0) == 0
-        return sums, jnp.where(first, sums, squares)
+        return sums, jnp.concatenate([sums, squares], axis=0)
 
     def reduce_start(layer, mine):
         st_tx[layer, 0] = mine
         for step in range(1, 8):
             stat_copy(layer, 0, step).start()
 
-    def reduce_finish(layer, mine):
+    def sent(layer):
+        for face in range(FACES):
+            halo_copy(layer, face).wait_send()
+            return_copy(layer, face, n_dev - offsets[face]).wait_send()
+        for step in range(1, 8):
+            stat_copy(layer, 0, step).wait_send()
+        if layer == 1:
+            for step in range(1, n_high):
+                stat_copy(0, 1, step).wait_send()
+
+            @pl.loop(0, PAIRS * blocks)
+            def _(step):
+                out_copy(lax.div(step, blocks), lax.rem(step, blocks)).wait()
+
+    def reduce_finish(layer, mine, beside):
         for step in range(1, 8):
             stat_copy(layer, 0, step).wait_recv()
         for step in range(1, 8):
@@ -436,6 +450,7 @@
         st_tx[layer, 1] = mine
         for step in range(1, n_high):
             stat_copy(layer, 1, step).start()
+        beside()
         for step in range(1, n_high):
             stat_copy(layer, 1, step).wait_recv()
         for step in range(1, n_high):
@@ -446,6 +461,7 @@
         mult = ng[layer : layer + 1, :] * lax.rsqrt(var + 1e-05)
         return mu, mult, ns[layer : layer + 1, :]
 
+    clear()
     edge_layer(0, None)
     sums, mine = node_layer(0)
     reduce_start(0, mine)
@@ -458,7 +474,8 @@
         tx1[face, H : H + REF, :] = jnp.broadcast_to(ref_wide, (REF, T)).astype(BF16)
     for face in SEQUENCE:
         halo_copy(1, face).start()
-    mu, mult, shift = reduce_finish(0, mine)
+    clear()
+    mu, mult, shift = reduce_finish(0, mine, functools.partial(sent, 0))
 
     @pl.loop(0, groups // 2, unroll=4)
     def _(step):
@@ -471,7 +488,7 @@
     edge_layer(1, (mu, mult, shift))
     _, mine = node_layer(1)
     reduce_start(1, mine)
-    mu, mult, shift = reduce_finish(1, mine)
+    mu, mult, shift = reduce_finish(1, mine, functools.partial(sent, 1))
 
     @pl.loop(0, nodes // ROWS)
     def _(step):
@@ -482,18 +499,8 @@
     node_copy = pltpu.make_async_copy(hb, node_out, node_sem)
     node_copy.start()
 
-    @pl.loop(0, PAIRS * blocks)
-    def _(step):
-        out_copy(lax.div(step, blocks), lax.rem(step, blocks)).wait()
-
-    for layer in range(LAYERS):
-        for face in range(FACES):
-            halo_copy(layer, face).wait_send()
-            return_copy(layer, face, n_dev - offsets[face]).wait_send()
-        for step in range(1, 8):
-            stat_copy(layer, 0, step).wait_send()
-        for step in range(1, n_high):
-            stat_copy(layer, 1, step).wait_send()
+    for step in range(1, n_high):
+        stat_copy(1, 1, step).wait_send()
 
     node_copy.wait()
 
@@ -545,9 +552,9 @@
             pltpu.VMEM((LAYERS, FACES, H, T), BF16),
             pltpu.VMEM((LAYERS, 4, T, T), BF16),
             pltpu.VMEM((LAYERS, 3, T, T), F32),
-            pltpu.VMEM((LAYERS, 2, 8, T), F32),
-            pltpu.VMEM((LAYERS, 7, 8, T), F32),
-            pltpu.VMEM((LAYERS, n_high - 1, 8, T), F32),
+            pltpu.VMEM((LAYERS, 2, 2, T), F32),
+            pltpu.VMEM((LAYERS, 7, 2, T), F32),
+            pltpu.VMEM((LAYERS, n_high - 1, 2, T), F32),
             dma((n_copies,)),
             dma((n_copies,)),
             dma((LAYERS, FACES)),

time: 91.4 us -> 90 us (0.985)
  Pallas kernels: 86.9 us -> 85.6 us
    pallas_call x1, Pallas kernels: 86.9 us -> 85.6 us  [per_device(): pl.pallas_call(functools.partial(kernel, n_dev, groups), out_shape=(pltpu...]
where the time goes in v4:
time: 90 us; the launch traced here: 89.9 us
  Pallas kernels  85.6 us (95%)
  local copies, waits for them, and re-layouts  3.68 us (4%)
    pallas_call x1, Pallas kernels, per_device(): pl.pallas_call(functools.partial(kernel, n_dev, groups), out_shape=(pltpu...  85.6 us
    unnamed x2, local copies, waits for them, and re-layouts  3.68 us

profile of v4, /device:TPU:1, one launch (start us, length us, event | category | flops | bytes accessed | tf_op | source)
XLA Modules:
  0.0 89.9 jit_solution(17220917581752147727)
XLA Ops:
  0.6 85.6 %shard_map.158 = (bf16[4096,128]{1,0:T(8,128)(2,1)S(1)}, bf16[32,6,128,128]{3,2,1,0:T(8,128)(2,1)S(1)}) custom-call(bf16[4096,128]{1,0:T(8,128)(2,1)} %node_ref.1, bf16[32,6,128,128]{3,2,1,0:T(8,128)(2,1)} %bitcast.5, s32[2,24576]{1,0:T(2,128)} %ends_ref.1, s32[1,24576]{1,0:T(1,128)} %bitcast.6, s32[6,1,256]{2,1,0:T(1,128)} %bitcast.7, ...), custom_call_target="tpu_custom_call" | custom-call | tf_op jit(solution)/shard_map/pallas_call | solution.py:526
  86.2 1.0 %copy.19 = bf16[4096,128]{1,0:T(8,128)(2,1)} copy(bf16[4096,128]{1,0:T(8,128)(2,1)S(1)} %get-tuple-element.6) | data formatting | bytes 2097152
  87.2 2.7 %copy.20 = bf16[24576,128]{1,0:T(8,128)(2,1)} copy(bf16[24576,128]{1,0:T(8,128)(2,1)S(1)} %bitcast.4) | data formatting | bytes 12582912
